TPU v7x, 8 devices: a whole 2x2x1 slice. The times are simulated.
8 devices in a mesh: rep: 1 (over z), data: 2 (over y), stage: 4 (over x, core).
Axes of the slice: x: 2, y: 2, z: 1, core: 2. Of those that a mesh axis runs over, the one named last changes fastest.
Arguments:
- embeds: bfloat16 [8, 2, 384, 1536], P(('rep', 'data'))
- targets: bfloat16 [8, 2, 384, 1536], P(('rep', 'data'))
- w_qkv: bfloat16 [4, 3, 16, 96, 1536], P(('rep', 'stage'))
- w_out: bfloat16 [4, 16, 96, 1536], P(('rep', 'stage'))
- w_up: bfloat16 [4, 1536, 6144], P(('rep', 'stage'))
- w_down: bfloat16 [4, 6144, 1536], P(('rep', 'stage'))
Outputs:
- output 1: float32 [1], P('rep')
- output 2: float32 [4, 3, 16, 96, 1536], P(('rep', 'stage'))
- output 3: float32 [4, 16, 96, 1536], P(('rep', 'stage'))
- output 4: float32 [4, 1536, 6144], P(('rep', 'stage'))
- output 5: float32 [4, 6144, 1536], P(('rep', 'stage'))
- output 6: bfloat16 [8, 2, 384, 1536], P(('rep', 'data'))
All inputs are finite; a program needn't handle non-finite values.
Results may differ from a plain program's by a relative error of at most 0.0170999.
Values are sent between devices in bfloat16 or wider.
A program may use at most 1 GiB of HBM per device.

v0:
```python
import jax
import jax.numpy as jnp
from jax import lax
from jax.sharding import PartitionSpec as P

NORM_EPS = 1e-6


def rms_norm(vals):
    return vals * lax.rsqrt(jnp.mean(vals * vals, axis=-1, keepdims=True) + NORM_EPS)


def gelu_tanh(vals):
    return jax.nn.gelu(vals, approximate=True)


def layer_forward(act_in, w_qkv, w_out, w_up, w_down):
    seq_len = act_in.shape[1]
    scale = w_qkv.shape[2] ** -0.5
    act32 = act_in.astype(jnp.float32)
    normed1 = rms_norm(act32).astype(jnp.bfloat16)
    qkv_proj = jnp.einsum('bsd,thkd->tbhsk', normed1, w_qkv, preferred_element_type=jnp.float32).astype(jnp.bfloat16)
    query = qkv_proj[0]
    keys = qkv_proj[1]
    values = qkv_proj[2]
    scores = jnp.einsum('bhqk,bhsk->bhqs', query, keys, preferred_element_type=jnp.float32) * scale
    causal = lax.broadcasted_iota(jnp.int32, (seq_len, seq_len), 0) >= lax.broadcasted_iota(jnp.int32, (seq_len, seq_len), 1)
    probs32 = jax.nn.softmax(jnp.where(causal, scores, -1e30), axis=-1)
    attn_probs = probs32.astype(jnp.bfloat16)
    context = jnp.einsum('bhqs,bhsk->bhqk', attn_probs, values, preferred_element_type=jnp.float32).astype(jnp.bfloat16)
    attn_out = jnp.einsum('cirl,ile->cre', context, w_out, preferred_element_type=jnp.float32)
    hidden32 = (act32 + attn_out).astype(jnp.bfloat16).astype(jnp.float32)
    normed2 = rms_norm(hidden32).astype(jnp.bfloat16)
    pre_act = jnp.einsum('bsd,df->bsf', normed2, w_up, preferred_element_type=jnp.float32)
    upper = gelu_tanh(pre_act).astype(jnp.bfloat16)
    mlp_out = jnp.einsum('bsf,fd->bsd', upper, w_down, preferred_element_type=jnp.float32)
    layer_out = (hidden32 + mlp_out).astype(jnp.bfloat16)
    saved = (act32, normed1, query, keys, values, probs32, attn_probs, context, hidden32, normed2, pre_act, upper)
    return layer_out, saved


def layer_backward(grad_out, saved, w_qkv, w_out, w_up, w_down):
    act32, normed1, query, keys, values, probs32, attn_probs, context, hidden32, normed2, pre_act, upper = saved
    scale = w_qkv.shape[2] ** -0.5
    d_down = jnp.einsum('bsf,bsd->fd', upper, grad_out, preferred_element_type=jnp.float32)
    d_upper = jnp.einsum('bsd,fd->bsf', grad_out, w_down, preferred_element_type=jnp.float32)
    d_pre = jax.vjp(gelu_tanh, pre_act)[1](d_upper)[0].astype(jnp.bfloat16)
    d_up = jnp.einsum('bsd,bsf->df', normed2, d_pre, preferred_element_type=jnp.float32)
    d_normed2 = jnp.einsum('bsf,df->bsd', d_pre, w_up, preferred_element_type=jnp.float32)
    d_hidden = grad_out.astype(jnp.float32) + jax.vjp(rms_norm, hidden32)[1](d_normed2)[0]
    d_hidden16 = d_hidden.astype(jnp.bfloat16)
    d_out = jnp.einsum('cirl,cre->ile', context, d_hidden16, preferred_element_type=jnp.float32)
    d_context = jnp.einsum('cre,ile->cirl', d_hidden16, w_out, preferred_element_type=jnp.float32).astype(jnp.bfloat16)
    d_probs = jnp.einsum('bhqk,bhsk->bhqs', d_context, values, preferred_element_type=jnp.float32)
    d_values = jnp.einsum('bhqs,bhqk->bhsk', attn_probs, d_context, preferred_element_type=jnp.float32)
    d_scores = (probs32 * (d_probs - jnp.sum(d_probs * probs32, axis=-1, keepdims=True)) * scale).astype(jnp.bfloat16)
    d_query = jnp.einsum('bhqs,bhsk->bhqk', d_scores, keys, preferred_element_type=jnp.float32)
    d_keys = jnp.einsum('bhqs,bhqk->bhsk', d_scores, query, preferred_element_type=jnp.float32)
    d_qkv = jnp.stack([d_query, d_keys, d_values]).astype(jnp.bfloat16)
    d_qkv_w = jnp.einsum('tbhsk,bsd->thkd', d_qkv, normed1, preferred_element_type=jnp.float32)
    d_normed1 = jnp.einsum('tbhsk,thkd->bsd', d_qkv, w_qkv, preferred_element_type=jnp.float32)
    d_act = d_hidden + jax.vjp(rms_norm, act32)[1](d_normed1)[0]
    return d_act.astype(jnp.bfloat16), (d_qkv_w, d_out, d_up, d_down)


def solution(mesh):
    n_stages = mesh.shape['stage']
    n_data = mesh.shape['data']
    next_pairs = [(src, src + 1) for src in range(n_stages - 1)]
    prev_pairs = [(src + 1, src) for src in range(n_stages - 1)]
    act_spec = P(('rep', 'data'))
    weight_spec = P(('rep', 'stage'))

    def per_device(embeds, targets, w_qkv, w_out, w_up, w_down):
        weights = (w_qkv[0], w_out[0], w_up[0], w_down[0])
        n_micro, micro_b, seq_len, width = embeds.shape
        stage_idx = lax.axis_index('stage')
        is_first = stage_idx == 0
        is_last = stage_idx == n_stages - 1
        grad_scale = 1.0 / (n_data * n_micro)
        loss_norm = 1.0 / (n_data * n_micro * micro_b * seq_len * width)

        def run_forward(act_in):
            return layer_forward(act_in, *weights)[0]

        def skip_forward(act_in):
            return jnp.zeros_like(act_in)

        def run_backward(operands):
            act_in, grad_out = operands
            saved = layer_forward(act_in, *weights)[1]
            return layer_backward(grad_out, saved, *weights)

        def skip_backward(operands):
            return jnp.zeros_like(operands[0]), tuple(jnp.zeros(w.shape, jnp.float32) for w in weights)

        def tick_body(tick, carry):
            from_prev, from_next, stash, grad_sums, dx_buf, loss_sum = carry
            fwd_micro = tick - stage_idx
            fwd_valid = (fwd_micro >= 0) & (fwd_micro < n_micro)
            fwd_slot = jnp.clip(fwd_micro, 0, n_micro - 1)
            act_in = jnp.where(is_first, lax.dynamic_index_in_dim(embeds, fwd_slot, 0, keepdims=False), from_prev)
            act_out = lax.cond(fwd_valid, run_forward, skip_forward, act_in)
            kept = lax.dynamic_index_in_dim(stash, fwd_slot, 0, keepdims=False)
            stash = lax.dynamic_update_index_in_dim(stash, jnp.where(fwd_valid, act_in, kept), fwd_slot, 0)
            target_mb = lax.dynamic_index_in_dim(targets, fwd_slot, 0, keepdims=False)
            error_mb = act_out.astype(jnp.float32) - target_mb.astype(jnp.float32)
            loss_mb = 0.5 * jnp.sum(error_mb * error_mb) * loss_norm
            loss_sum = loss_sum + jnp.where(is_last & fwd_valid, loss_mb, 0.0)
            grad_seed = (error_mb * grad_scale).astype(jnp.bfloat16)
            bwd_micro = tick + stage_idx - (2 * n_stages - 2)
            bwd_valid = (bwd_micro >= 0) & (bwd_micro < n_micro)
            bwd_slot = jnp.clip(bwd_micro, 0, n_micro - 1)
            grad_out = jnp.where(is_last, grad_seed, from_next)
            act_saved = lax.dynamic_index_in_dim(stash, bwd_slot, 0, keepdims=False)
            grad_in, layer_grads = lax.cond(bwd_valid, run_backward, skip_backward, (act_saved, grad_out))
            grad_sums = tuple(total + piece for total, piece in zip(grad_sums, layer_grads))
            old_dx = lax.dynamic_index_in_dim(dx_buf, bwd_slot, 0, keepdims=False)
            dx_buf = lax.dynamic_update_index_in_dim(dx_buf, jnp.where(is_first & bwd_valid, grad_in, old_dx), bwd_slot, 0)
            from_prev = lax.ppermute(act_out, 'stage', next_pairs)
            from_next = lax.ppermute(grad_in, 'stage', prev_pairs)
            return from_prev, from_next, stash, grad_sums, dx_buf, loss_sum

        micro_zeros = jnp.zeros((micro_b, seq_len, width), jnp.bfloat16)
        init_carry = (micro_zeros, micro_zeros, jnp.zeros_like(embeds), tuple(jnp.zeros(w.shape, jnp.float32) for w in weights), jnp.zeros_like(embeds), jnp.zeros((), jnp.float32))
        n_ticks = n_micro + 2 * n_stages - 2
        final_carry = lax.fori_loop(0, n_ticks, tick_body, init_carry)
        grad_sums = final_carry[3]
        dx_buf = final_carry[4]
        loss_sum = final_carry[5]
        loss = lax.psum(loss_sum, ('data', 'stage')).reshape(1)
        d_weights = tuple(lax.psum(total, 'data')[None] for total in grad_sums)
        d_embeds = lax.psum(dx_buf, 'stage')
        return (loss,) + d_weights + (d_embeds,)

    return jax.shard_map(per_device, mesh=mesh, in_specs=(act_spec, act_spec, weight_spec, weight_spec, weight_spec, weight_spec), out_specs=(P('rep'), weight_spec, weight_spec, weight_spec, weight_spec, act_spec), check_vma=False)
```

profile of v0, /device:TPU:0, one launch (start us, length us, event | category | flops | bytes accessed | tf_op | source)
XLA Modules:
  0.0 7311.5 jit_solution(2975619087654762022)
XLA Ops:
  30.0 4575.6 %while.32 = (s32[]{:T(128)}, bf16[2,384,1536]{2,1,0:T(8,128)(2,1)}, bf16[2,384,1536]{2,1,0:T(8,128)(2,1)}, bf16[4,2,384,1536]{3,2,1,0:T(8,128)(2,1)}, f32[3,16,9...) while((s32[]{:T(128)}, bf16[2,384,1536]{2,1,0:T(8,128)(2,1)}, ...), condition=%wide.region_17.18_spmd.clone, body=%wide.region_0.17_spmd.clone.sunk | while | flops 167198916608 | bytes 1490285696 | solution.py:127
  36.0 103.3 %conditional.6 = (bf16[2,384,1536]{2,1,0:T(8,128)(2,1)}, f32[2,384,1536]{2,1,0:T(8,128)}) conditional(s32[]{:T(128)} %convert_element_type.291, () %tuple.87, (bf16[2,384,1536]{2,1,0:T(8,128)(2,1)S(1)}, bf16[3,16,96,1536]{3,2,0,1:T(8,128)(2,1)}, bf16[16,96,1536]{2,1,0:T(8,128)(2,1)}, bf16[1536,6144]{1,0:T(8,128)(2,1)}, ...), branch_computations={%region_1.1_spmd, %region_2.6_spmd} | conditional | flops 45405978624 | bytes 224550992 | solution.py:103
  144.3 49.6 conditional.7
  295.0 102.7 %conditional.6 = (bf16[2,384,1536]{2,1,0:T(8,128)(2,1)}, f32[2,384,1536]{2,1,0:T(8,128)}) conditional(s32[]{:T(128)} %convert_element_type.291, () %tuple.87, (bf16[2,384,1536]{2,1,0:T(8,128)(2,1)S(1)}, bf16[3,16,96,1536]{3,2,0,1:T(8,128)(2,1)}, bf16[16,96,1536]{2,1,0:T(8,128)(2,1)}, bf16[1536,6144]{1,0:T(8,128)(2,1)}, ...), branch_computations={%region_1.1_spmd, %region_2.6_spmd} | conditional | flops 45405978624 | bytes 224550992 | solution.py:103
  402.7 49.9 conditional.7
  458.3 38.1 select_add_fusion.10
  496.5 38.1 select_add_fusion.11
  534.5 27.8 select_add_fusion.8
  587.3 103.0 %conditional.6 = (bf16[2,384,1536]{2,1,0:T(8,128)(2,1)}, f32[2,384,1536]{2,1,0:T(8,128)}) conditional(s32[]{:T(128)} %convert_element_type.291, () %tuple.87, (bf16[2,384,1536]{2,1,0:T(8,128)(2,1)S(1)}, bf16[3,16,96,1536]{3,2,0,1:T(8,128)(2,1)}, bf16[16,96,1536]{2,1,0:T(8,128)(2,1)}, bf16[1536,6144]{1,0:T(8,128)(2,1)}, ...), branch_computations={%region_1.1_spmd, %region_2.6_spmd} | conditional | flops 45405978624 | bytes 224550992 | solution.py:103
  695.3 49.6 conditional.7
  750.6 38.1 select_add_fusion.10
  788.8 38.1 select_add_fusion.11
  826.9 27.8 select_add_fusion.8
  879.9 102.7 %conditional.6 = (bf16[2,384,1536]{2,1,0:T(8,128)(2,1)}, f32[2,384,1536]{2,1,0:T(8,128)}) conditional(s32[]{:T(128)} %convert_element_type.291, () %tuple.87, (bf16[2,384,1536]{2,1,0:T(8,128)(2,1)S(1)}, bf16[3,16,96,1536]{3,2,0,1:T(8,128)(2,1)}, bf16[16,96,1536]{2,1,0:T(8,128)(2,1)}, bf16[1536,6144]{1,0:T(8,128)(2,1)}, ...), branch_computations={%region_1.1_spmd, %region_2.6_spmd} | conditional | flops 45405978624 | bytes 224550992 | solution.py:103
  987.6 49.9 conditional.7
  1043.3 38.1 select_add_fusion.10
  1081.4 38.1 select_add_fusion.11
  1119.5 27.8 select_add_fusion.8
  1186.0 49.6 conditional.7
  1237.0 99.2 %collective-permute-start = (bf16[2,384,1536]{2,1,0:T(8,128)(2,1)}, bf16[2,384,1536]{2,1,0:T(8,128)(2,1)}, u32[]{:S(2)}, u32[]{:S(2)}) collective-permute-start(bf16[2,384,1536]{2,1,0:T(8,128)(2,1)} %get-tuple-element.800), channel_id=1, source_target_pairs={{0,1},{1,2},{2,3},{4,5},{5,6},{6,7}} | collective-permute-start | bytes 7077896 | tf_op jit(solution)/shard_map/while/body/eval_jaxpr/ppermute | solution.py:120
  1336.2 38.1 select_add_fusion.10
  1374.3 38.1 select_add_fusion.11
  1412.4 27.8 select_add_fusion.8
  1479.0 49.9 conditional.7
  1530.1 843.1 %collective-permute-start = (bf16[2,384,1536]{2,1,0:T(8,128)(2,1)}, bf16[2,384,1536]{2,1,0:T(8,128)(2,1)}, u32[]{:S(2)}, u32[]{:S(2)}) collective-permute-start(bf16[2,384,1536]{2,1,0:T(8,128)(2,1)} %get-tuple-element.800), channel_id=1, source_target_pairs={{0,1},{1,2},{2,3},{4,5},{5,6},{6,7}} | collective-permute-start | bytes 7077896 | tf_op jit(solution)/shard_map/while/body/eval_jaxpr/ppermute | solution.py:120
  2373.3 38.1 select_add_fusion.10
  2411.4 38.1 select_add_fusion.11
  2449.5 27.8 select_add_fusion.8
  2516.0 331.1 %conditional.7 = (bf16[2,384,1536]{2,1,0:T(8,128)(2,1)}, f32[3,16,96,1536]{3,2,1,0:T(8,128)}, f32[16,96,1536]{2,1,0:T(8,128)}, f32[1536,6144]{1,0:T(8,128)}, f32[6144,1536]{1,0:T(8,128)}) conditional(s32[]{:T(128)} %convert_element_type.292, () %tuple.89, (pred[]{:T(512)}, bf16[2,384,1536]{2,1,0:T(8,128)(2,1)S(1)}, bf16[2,384,1536]{2,1,0:T(8,128)(2,1)}, ...), branch_computations={%region_7.7_spmd, %region_8.15_spmd} | conditional | flops 121725698048 | bytes 859934144 | solution.py:116
  2607.1 31.4 fusion.70
  2705.6 29.8 convert_bitcast_fusion.4
  2735.4 29.4 convert_bitcast_fusion.3
  2820.1 26.6 convolution_bitcast_fusion.1
  2848.4 98.0 %collective-permute-start = (bf16[2,384,1536]{2,1,0:T(8,128)(2,1)}, bf16[2,384,1536]{2,1,0:T(8,128)(2,1)}, u32[]{:S(2)}, u32[]{:S(2)}) collective-permute-start(bf16[2,384,1536]{2,1,0:T(8,128)(2,1)} %get-tuple-element.800), channel_id=1, source_target_pairs={{0,1},{1,2},{2,3},{4,5},{5,6},{6,7}} | collective-permute-start | bytes 7077896 | tf_op jit(solution)/shard_map/while/body/eval_jaxpr/ppermute | solution.py:120
  2946.4 38.1 select_add_fusion.10
  2984.5 38.1 select_add_fusion.11
  3022.6 27.8 select_add_fusion.8
  3090.8 331.0 %conditional.7 = (bf16[2,384,1536]{2,1,0:T(8,128)(2,1)}, f32[3,16,96,1536]{3,2,1,0:T(8,128)}, f32[16,96,1536]{2,1,0:T(8,128)}, f32[1536,6144]{1,0:T(8,128)}, f32[6144,1536]{1,0:T(8,128)}) conditional(s32[]{:T(128)} %convert_element_type.292, () %tuple.89, (pred[]{:T(512)}, bf16[2,384,1536]{2,1,0:T(8,128)(2,1)S(1)}, bf16[2,384,1536]{2,1,0:T(8,128)(2,1)}, ...), branch_computations={%region_7.7_spmd, %region_8.15_spmd} | conditional | flops 121725698048 | bytes 859934144 | solution.py:116
  3181.8 31.4 fusion.70
  3280.4 29.8 convert_bitcast_fusion.4
  3310.2 29.4 convert_bitcast_fusion.3
  3394.8 26.6 convolution_bitcast_fusion.1
  3427.6 38.1 select_add_fusion.10
  3465.7 38.1 select_add_fusion.11
  3503.8 27.8 select_add_fusion.8
  3572.0 331.0 %conditional.7 = (bf16[2,384,1536]{2,1,0:T(8,128)(2,1)}, f32[3,16,96,1536]{3,2,1,0:T(8,128)}, f32[16,96,1536]{2,1,0:T(8,128)}, f32[1536,6144]{1,0:T(8,128)}, f32[6144,1536]{1,0:T(8,128)}) conditional(s32[]{:T(128)} %convert_element_type.292, () %tuple.89, (pred[]{:T(512)}, bf16[2,384,1536]{2,1,0:T(8,128)(2,1)S(1)}, bf16[2,384,1536]{2,1,0:T(8,128)(2,1)}, ...), branch_computations={%region_7.7_spmd, %region_8.15_spmd} | conditional | flops 121725698048 | bytes 859934144 | solution.py:116
  3662.9 31.4 fusion.70
  3761.5 29.8 convert_bitcast_fusion.4
  3791.3 29.4 convert_bitcast_fusion.3
  3875.9 26.6 convolution_bitcast_fusion.1
  3904.2 92.8 %collective-permute-start = (bf16[2,384,1536]{2,1,0:T(8,128)(2,1)}, bf16[2,384,1536]{2,1,0:T(8,128)(2,1)}, u32[]{:S(2)}, u32[]{:S(2)}) collective-permute-start(bf16[2,384,1536]{2,1,0:T(8,128)(2,1)} %get-tuple-element.800), channel_id=1, source_target_pairs={{0,1},{1,2},{2,3},{4,5},{5,6},{6,7}} | collective-permute-start | bytes 7077896 | tf_op jit(solution)/shard_map/while/body/eval_jaxpr/ppermute | solution.py:120
  3997.0 38.1 select_add_fusion.10
  4035.1 38.1 select_add_fusion.11
  4073.2 27.8 select_add_fusion.8
  4141.5 331.0 %conditional.7 = (bf16[2,384,1536]{2,1,0:T(8,128)(2,1)}, f32[3,16,96,1536]{3,2,1,0:T(8,128)}, f32[16,96,1536]{2,1,0:T(8,128)}, f32[1536,6144]{1,0:T(8,128)}, f32[6144,1536]{1,0:T(8,128)}) conditional(s32[]{:T(128)} %convert_element_type.292, () %tuple.89, (pred[]{:T(512)}, bf16[2,384,1536]{2,1,0:T(8,128)(2,1)S(1)}, bf16[2,384,1536]{2,1,0:T(8,128)(2,1)}, ...), branch_computations={%region_7.7_spmd, %region_8.15_spmd} | conditional | flops 121725698048 | bytes 859934144 | solution.py:116
  4232.4 31.4 fusion.70
  4331.0 29.8 convert_bitcast_fusion.4
  4360.8 29.4 convert_bitcast_fusion.3
  4478.2 38.1 select_add_fusion.10
  4516.3 38.1 select_add_fusion.11
  4554.4 27.8 select_add_fusion.8
  4631.5 141.7 %all-reduce.4.cloned.1.call-done = bf16[4,2,384,1536]{3,2,1,0:T(8,128)(2,1)} async-done(((bf16[4,2,384,1536]{3,2,1,0:T(8,128)(2,1)}), bf16[4,2,384,1536]{3,2,1,0:T(8,128)(2,1)}) %all-reduce.4.cloned.1.call-update) | async-done | bytes 9437200 | tf_op jit(solution)/shard_map/psum | solution.py:133
  4773.1 2447.5 %all-reduce.6.cloned.1.call-done = (f32[1,3,16,96,1536]{4,3,2,1,0:T(8,128)}, f32[1,16,96,1536]{3,2,1,0:T(8,128)}, f32[1,1536,6144]{2,1,0:T(8,128)}, f32[1,6144,1536]{2,1,0:T(8,128)}) async-done(((f32[1,3,16,96,1536]{4,3,2,1,0:T(8,128)}, f32[1,16,96,1536]{3,2,1,0:T(8,128)}, f32[1,1536,6144]{2,1,0:T(8,128)}, f32[1,6144,1536]{2,1,0:T(8,128)}), (f32[1,3,16,96,1536]{4,3,2,1,0:T(8,128)}, ...) | async-done | bytes 113246224 | tf_op jit(solution)/shard_map/psum | solution.py:132
  7250.0 31.6 copy.112
  (525 shorter events, 2143.4 us)
Async XLA Ops:
  7.2 4766.0 %all-reduce.4.cloned.1.call-start = ((), (), s32[]{:S(2)}) async-start(), calls=%async_computation | async-start | bytes 18874368 | tf_op jit(solution)/shard_map/psum | solution.py:133
  95.3 24.0 copy-start.21
  193.9 93.2 %collective-permute-start.1 = (bf16[2,384,1536]{2,1,0:T(8,128)(2,1)}, bf16[2,384,1536]{2,1,0:T(8,128)(2,1)S(1)}, u32[]{:S(2)}, u32[]{:S(2)}) collective-permute-start(bf16[2,384,1536]{2,1,0:T(8,128)(2,1)} %get-tuple-element.804), channel_id=1, source_target_pairs={{1,0},{2,1},{3,2},{5,4},{6,5},{7,6}} | collective-permute-start | bytes 7077896 | tf_op jit(solution)/shard_map/while/body/eval_jaxpr/ppermute | solution.py:121
  195.2 91.9 %collective-permute-start = (bf16[2,384,1536]{2,1,0:T(8,128)(2,1)}, bf16[2,384,1536]{2,1,0:T(8,128)(2,1)}, u32[]{:S(2)}, u32[]{:S(2)}) collective-permute-start(bf16[2,384,1536]{2,1,0:T(8,128)(2,1)} %get-tuple-element.800), channel_id=1, source_target_pairs={{0,1},{1,2},{2,3},{4,5},{5,6},{6,7}} | collective-permute-start | bytes 7077896 | tf_op jit(solution)/shard_map/while/body/eval_jaxpr/ppermute | solution.py:120
  354.2 23.8 copy-start.21
  452.6 127.1 %collective-permute-start.1 = (bf16[2,384,1536]{2,1,0:T(8,128)(2,1)}, bf16[2,384,1536]{2,1,0:T(8,128)(2,1)S(1)}, u32[]{:S(2)}, u32[]{:S(2)}) collective-permute-start(bf16[2,384,1536]{2,1,0:T(8,128)(2,1)} %get-tuple-element.804), channel_id=1, source_target_pairs={{1,0},{2,1},{3,2},{5,4},{6,5},{7,6}} | collective-permute-start | bytes 7077896 | tf_op jit(solution)/shard_map/while/body/eval_jaxpr/ppermute | solution.py:121
  453.9 125.8 %collective-permute-start = (bf16[2,384,1536]{2,1,0:T(8,128)(2,1)}, bf16[2,384,1536]{2,1,0:T(8,128)(2,1)}, u32[]{:S(2)}, u32[]{:S(2)}) collective-permute-start(bf16[2,384,1536]{2,1,0:T(8,128)(2,1)} %get-tuple-element.800), channel_id=1, source_target_pairs={{0,1},{1,2},{2,3},{4,5},{5,6},{6,7}} | collective-permute-start | bytes 7077896 | tf_op jit(solution)/shard_map/while/body/eval_jaxpr/ppermute | solution.py:120
  646.6 23.9 copy-start.21
  744.9 127.1 %collective-permute-start.1 = (bf16[2,384,1536]{2,1,0:T(8,128)(2,1)}, bf16[2,384,1536]{2,1,0:T(8,128)(2,1)S(1)}, u32[]{:S(2)}, u32[]{:S(2)}) collective-permute-start(bf16[2,384,1536]{2,1,0:T(8,128)(2,1)} %get-tuple-element.804), channel_id=1, source_target_pairs={{1,0},{2,1},{3,2},{5,4},{6,5},{7,6}} | collective-permute-start | bytes 7077896 | tf_op jit(solution)/shard_map/while/body/eval_jaxpr/ppermute | solution.py:121
  746.2 125.8 %collective-permute-start = (bf16[2,384,1536]{2,1,0:T(8,128)(2,1)}, bf16[2,384,1536]{2,1,0:T(8,128)(2,1)}, u32[]{:S(2)}, u32[]{:S(2)}) collective-permute-start(bf16[2,384,1536]{2,1,0:T(8,128)(2,1)} %get-tuple-element.800), channel_id=1, source_target_pairs={{0,1},{1,2},{2,3},{4,5},{5,6},{6,7}} | collective-permute-start | bytes 7077896 | tf_op jit(solution)/shard_map/while/body/eval_jaxpr/ppermute | solution.py:120
  939.1 23.8 copy-start.21
  1037.5 127.1 %collective-permute-start.1 = (bf16[2,384,1536]{2,1,0:T(8,128)(2,1)}, bf16[2,384,1536]{2,1,0:T(8,128)(2,1)S(1)}, u32[]{:S(2)}, u32[]{:S(2)}) collective-permute-start(bf16[2,384,1536]{2,1,0:T(8,128)(2,1)} %get-tuple-element.804), channel_id=1, source_target_pairs={{1,0},{2,1},{3,2},{5,4},{6,5},{7,6}} | collective-permute-start | bytes 7077896 | tf_op jit(solution)/shard_map/while/body/eval_jaxpr/ppermute | solution.py:121
  1038.8 125.8 %collective-permute-start = (bf16[2,384,1536]{2,1,0:T(8,128)(2,1)}, bf16[2,384,1536]{2,1,0:T(8,128)(2,1)}, u32[]{:S(2)}, u32[]{:S(2)}) collective-permute-start(bf16[2,384,1536]{2,1,0:T(8,128)(2,1)} %get-tuple-element.800), channel_id=1, source_target_pairs={{0,1},{1,2},{2,3},{4,5},{5,6},{6,7}} | collective-permute-start | bytes 7077896 | tf_op jit(solution)/shard_map/while/body/eval_jaxpr/ppermute | solution.py:120
  1235.7 221.9 %collective-permute-start.1 = (bf16[2,384,1536]{2,1,0:T(8,128)(2,1)}, bf16[2,384,1536]{2,1,0:T(8,128)(2,1)S(1)}, u32[]{:S(2)}, u32[]{:S(2)}) collective-permute-start(bf16[2,384,1536]{2,1,0:T(8,128)(2,1)} %get-tuple-element.804), channel_id=1, source_target_pairs={{1,0},{2,1},{3,2},{5,4},{6,5},{7,6}} | collective-permute-start | bytes 7077896 | tf_op jit(solution)/shard_map/while/body/eval_jaxpr/ppermute | solution.py:121
  1237.0 220.6 %collective-permute-start = (bf16[2,384,1536]{2,1,0:T(8,128)(2,1)}, bf16[2,384,1536]{2,1,0:T(8,128)(2,1)}, u32[]{:S(2)}, u32[]{:S(2)}) collective-permute-start(bf16[2,384,1536]{2,1,0:T(8,128)(2,1)} %get-tuple-element.800), channel_id=1, source_target_pairs={{0,1},{1,2},{2,3},{4,5},{5,6},{6,7}} | collective-permute-start | bytes 7077896 | tf_op jit(solution)/shard_map/while/body/eval_jaxpr/ppermute | solution.py:120
  1528.8 965.8 %collective-permute-start.1 = (bf16[2,384,1536]{2,1,0:T(8,128)(2,1)}, bf16[2,384,1536]{2,1,0:T(8,128)(2,1)S(1)}, u32[]{:S(2)}, u32[]{:S(2)}) collective-permute-start(bf16[2,384,1536]{2,1,0:T(8,128)(2,1)} %get-tuple-element.804), channel_id=1, source_target_pairs={{1,0},{2,1},{3,2},{5,4},{6,5},{7,6}} | collective-permute-start | bytes 7077896 | tf_op jit(solution)/shard_map/while/body/eval_jaxpr/ppermute | solution.py:121
  1530.1 964.5 %collective-permute-start = (bf16[2,384,1536]{2,1,0:T(8,128)(2,1)}, bf16[2,384,1536]{2,1,0:T(8,128)(2,1)}, u32[]{:S(2)}, u32[]{:S(2)}) collective-permute-start(bf16[2,384,1536]{2,1,0:T(8,128)(2,1)} %get-tuple-element.800), channel_id=1, source_target_pairs={{0,1},{1,2},{2,3},{4,5},{5,6},{6,7}} | collective-permute-start | bytes 7077896 | tf_op jit(solution)/shard_map/while/body/eval_jaxpr/ppermute | solution.py:120
  2575.4 30.0 copy-start.14
  2583.5 21.9 copy-start.7
  2583.5 21.9 copy-start.3
  2607.0 31.4 copy-start.8
  2638.5 24.0 copy-start.9
  2662.5 19.7 copy-start.1
  2764.8 26.6 slice-start
  2797.9 18.0 copy-start.11
  2847.1 222.3 %collective-permute-start.1 = (bf16[2,384,1536]{2,1,0:T(8,128)(2,1)}, bf16[2,384,1536]{2,1,0:T(8,128)(2,1)S(1)}, u32[]{:S(2)}, u32[]{:S(2)}) collective-permute-start(bf16[2,384,1536]{2,1,0:T(8,128)(2,1)} %get-tuple-element.804), channel_id=1, source_target_pairs={{1,0},{2,1},{3,2},{5,4},{6,5},{7,6}} | collective-permute-start | bytes 7077896 | tf_op jit(solution)/shard_map/while/body/eval_jaxpr/ppermute | solution.py:121
  2848.4 221.0 %collective-permute-start = (bf16[2,384,1536]{2,1,0:T(8,128)(2,1)}, bf16[2,384,1536]{2,1,0:T(8,128)(2,1)}, u32[]{:S(2)}, u32[]{:S(2)}) collective-permute-start(bf16[2,384,1536]{2,1,0:T(8,128)(2,1)} %get-tuple-element.800), channel_id=1, source_target_pairs={{0,1},{1,2},{2,3},{4,5},{5,6},{6,7}} | collective-permute-start | bytes 7077896 | tf_op jit(solution)/shard_map/while/body/eval_jaxpr/ppermute | solution.py:120
  3150.2 29.9 copy-start.14
  3158.2 21.9 copy-start.7
  3158.3 21.9 copy-start.3
  3181.8 31.4 copy-start.8
  3213.2 24.0 copy-start.9
  3237.3 19.7 copy-start.1
  3339.6 26.6 slice-start
  3421.8 128.7 %collective-permute-start.1 = (bf16[2,384,1536]{2,1,0:T(8,128)(2,1)}, bf16[2,384,1536]{2,1,0:T(8,128)(2,1)S(1)}, u32[]{:S(2)}, u32[]{:S(2)}) collective-permute-start(bf16[2,384,1536]{2,1,0:T(8,128)(2,1)} %get-tuple-element.804), channel_id=1, source_target_pairs={{1,0},{2,1},{3,2},{5,4},{6,5},{7,6}} | collective-permute-start | bytes 7077896 | tf_op jit(solution)/shard_map/while/body/eval_jaxpr/ppermute | solution.py:121
  3423.1 127.5 %collective-permute-start = (bf16[2,384,1536]{2,1,0:T(8,128)(2,1)}, bf16[2,384,1536]{2,1,0:T(8,128)(2,1)}, u32[]{:S(2)}, u32[]{:S(2)}) collective-permute-start(bf16[2,384,1536]{2,1,0:T(8,128)(2,1)} %get-tuple-element.800), channel_id=1, source_target_pairs={{0,1},{1,2},{2,3},{4,5},{5,6},{6,7}} | collective-permute-start | bytes 7077896 | tf_op jit(solution)/shard_map/while/body/eval_jaxpr/ppermute | solution.py:120
  3631.4 29.9 copy-start.14
  3639.4 21.9 copy-start.7
  3639.4 21.9 copy-start.3
  3662.9 31.4 copy-start.8
  3694.4 24.0 copy-start.9
  3718.4 19.7 copy-start.1
  3820.7 26.6 slice-start
  3902.9 217.1 %collective-permute-start.1 = (bf16[2,384,1536]{2,1,0:T(8,128)(2,1)}, bf16[2,384,1536]{2,1,0:T(8,128)(2,1)S(1)}, u32[]{:S(2)}, u32[]{:S(2)}) collective-permute-start(bf16[2,384,1536]{2,1,0:T(8,128)(2,1)} %get-tuple-element.804), channel_id=1, source_target_pairs={{1,0},{2,1},{3,2},{5,4},{6,5},{7,6}} | collective-permute-start | bytes 7077896 | tf_op jit(solution)/shard_map/while/body/eval_jaxpr/ppermute | solution.py:121
  3904.2 215.8 %collective-permute-start = (bf16[2,384,1536]{2,1,0:T(8,128)(2,1)}, bf16[2,384,1536]{2,1,0:T(8,128)(2,1)}, u32[]{:S(2)}, u32[]{:S(2)}) collective-permute-start(bf16[2,384,1536]{2,1,0:T(8,128)(2,1)} %get-tuple-element.800), channel_id=1, source_target_pairs={{0,1},{1,2},{2,3},{4,5},{5,6},{6,7}} | collective-permute-start | bytes 7077896 | tf_op jit(solution)/shard_map/while/body/eval_jaxpr/ppermute | solution.py:120
  4200.9 29.9 copy-start.14
  4208.9 21.9 copy-start.7
  4208.9 21.9 copy-start.3
  4232.4 31.4 copy-start.8
  4263.9 24.0 copy-start.9
  4287.9 19.7 copy-start.1
  4390.2 26.6 slice-start
  4472.5 128.8 %collective-permute-start.1 = (bf16[2,384,1536]{2,1,0:T(8,128)(2,1)}, bf16[2,384,1536]{2,1,0:T(8,128)(2,1)S(1)}, u32[]{:S(2)}, u32[]{:S(2)}) collective-permute-start(bf16[2,384,1536]{2,1,0:T(8,128)(2,1)} %get-tuple-element.804), channel_id=1, source_target_pairs={{1,0},{2,1},{3,2},{5,4},{6,5},{7,6}} | collective-permute-start | bytes 7077896 | tf_op jit(solution)/shard_map/while/body/eval_jaxpr/ppermute | solution.py:121
  4473.8 127.5 %collective-permute-start = (bf16[2,384,1536]{2,1,0:T(8,128)(2,1)}, bf16[2,384,1536]{2,1,0:T(8,128)(2,1)}, u32[]{:S(2)}, u32[]{:S(2)}) collective-permute-start(bf16[2,384,1536]{2,1,0:T(8,128)(2,1)} %get-tuple-element.800), channel_id=1, source_target_pairs={{0,1},{1,2},{2,3},{4,5},{5,6},{6,7}} | collective-permute-start | bytes 7077896 | tf_op jit(solution)/shard_map/while/body/eval_jaxpr/ppermute | solution.py:120
  4605.6 2615.0 %all-reduce.6.cloned.1.call-start = ((), (), s32[]{:S(2)}) async-start(), calls=%async_computation.1 | async-start | bytes 226492416 | tf_op jit(solution)/shard_map/psum | solution.py:132
  7241.2 40.4 slice-start.2
  7241.2 40.4 slice-start.3
  7249.9 31.6 slice-start.4
  7249.9 31.6 slice-start.5
  7249.9 31.6 slice-start.6
  7249.9 31.6 slice-start.7
  7250.0 31.6 slice-start.8
  7250.0 31.6 slice-start.9
  7250.0 33.4 slice-start.10
  (69 other events, 554.9 us)
Sparse Core Ops, SparseCore 0:
  4605.7 167.3 all-reduce.3
  4776.4 2444.2 all-reduce.5
where the time goes:
time: 7320 us; the launch traced here: 7310 us
  waiting for transfers between devices  2590 us (35%)
  matrix products  1490 us (20%)
  other arithmetic  1480 us (20%)
  starting transfers between devices  1170 us (16%)
  local copies, waits for them, and re-layouts  472 us (6%)
  loops' own time  73.6 us (1%)
    psum x1, waiting for transfers between devices, per_device(): d_weights = tuple((lax.psum(total, 'data')[None] for total in grad_sums))  2450 us
    ppermute x10, starting transfers between devices, tick_body(): from_prev = lax.ppermute(act_out, 'stage', next_pairs)  1160 us
    add x40, other arithmetic, tick_body(): total + piece  1130 us
    another operation x46, local copies, waits for them, and re-layouts  306 us
    sub x8, other arithmetic, layer_forward(): probs32 = jax.nn.softmax(jnp.where(causal, scores, -1e+30), axis=-1)  184 us
    dot_general x8, matrix products, layer_forward(): jnp.einsum('bsd,df->bsf', normed2, w_up, preferred_element_type=jnp.float32)  183 us
  transfers between devices with their start and end apart: 22, of which 2 were waited for; matrix products, arithmetic and copies ran while one was open for 16% of the time, Pallas kernels for 0%

commit v1 on v0

v1 whole, which is shorter than its diff:
```python
import functools

import jax
import jax.numpy as jnp
from jax import lax
from jax.experimental import pallas as pl
from jax.experimental.pallas import tpu as pltpu
from jax.sharding import PartitionSpec as P


NORM_EPS = 1e-6
ROWS = 128


def rms_norm(vals):
    return vals * lax.rsqrt(jnp.mean(vals * vals, axis=-1, keepdims=True) + NORM_EPS)


def gelu_tanh(vals):
    return jax.nn.gelu(vals, approximate=True)


def dot_nn(lhs, rhs):
    return lax.dot_general(lhs, rhs, (((1,), (0,)), ((), ())), preferred_element_type=jnp.float32)


def dot_nt(lhs, rhs):
    return lax.dot_general(lhs, rhs, (((1,), (1,)), ((), ())), preferred_element_type=jnp.float32)


def dot_tn(lhs, rhs):
    return lax.dot_general(lhs, rhs, (((0,), (0,)), ((), ())), preferred_element_type=jnp.float32)


def empty_arrays(*specs):
    def kernel(*refs):
        del refs

    return pl.pallas_call(
        kernel,
        out_shape=[jax.ShapeDtypeStruct(shape, dtype) for shape, dtype in specs],
        out_specs=[pl.BlockSpec(memory_space=pl.ANY)] * len(specs),
        name='empty',
    )()


def row_probs(query, keys, row0, scale):
    scores = dot_nt(query, keys) * scale
    row_id = row0 + lax.broadcasted_iota(jnp.int32, scores.shape, 0)
    col_id = lax.broadcasted_iota(jnp.int32, scores.shape, 1)
    scores = jnp.where(row_id >= col_id, scores, -1e30)
    weights = jnp.exp(scores - jnp.max(scores, axis=-1, keepdims=True))
    return weights * (1.0 / jnp.sum(weights, axis=-1, keepdims=True))


def attn_fwd_kernel(head_dim, slot_ref, q_ref, k_ref, v_ref, old_ref, out_ref):
    del slot_ref, old_ref
    seq_len, lanes = q_ref.shape[1:]
    scale = head_dim ** -0.5
    for row0 in range(0, seq_len, ROWS):
        n_cols = row0 + ROWS
        pieces = []
        for lane0 in range(0, lanes, head_dim):
            head = slice(lane0, lane0 + head_dim)
            probs = row_probs(q_ref[0, row0:n_cols, head], k_ref[0, :n_cols, head], row0, scale)
            pieces.append(dot_nn(probs.astype(jnp.bfloat16), v_ref[0, :n_cols, head]).astype(jnp.bfloat16))
        out_ref[0, row0:n_cols, :] = jnp.concatenate(pieces, axis=1)


def attn_bwd_kernel(head_dim, n_groups, slot_ref, q_ref, k_ref, v_ref, dctx_ref, old_ref, out_ref):
    del slot_ref, old_ref
    seq_len, lanes = q_ref.shape[1:]
    scale = head_dim ** -0.5
    n_rows = seq_len // ROWS
    dq_rows = [[] for _ in range(n_rows)]
    dk_rows = [[] for _ in range(n_rows)]
    dv_rows = [[] for _ in range(n_rows)]
    for lane0 in range(0, lanes, head_dim):
        head = slice(lane0, lane0 + head_dim)
        dk_sum = [None] * n_rows
        dv_sum = [None] * n_rows
        for row_blk in range(n_rows):
            row0 = row_blk * ROWS
            n_cols = row0 + ROWS
            query = q_ref[0, row0:n_cols, head]
            keys = k_ref[0, :n_cols, head]
            dctx = dctx_ref[row0:n_cols, head]
            probs = row_probs(query, keys, row0, scale)
            d_probs = dot_nt(dctx, v_ref[0, :n_cols, head])
            delta = jnp.sum(d_probs * probs, axis=-1, keepdims=True)
            d_scores = (probs * (d_probs - delta) * scale).astype(jnp.bfloat16)
            dq_rows[row_blk].append(dot_nn(d_scores, keys).astype(jnp.bfloat16))
            dk_part = dot_tn(d_scores, query)
            dv_part = dot_tn(probs.astype(jnp.bfloat16), dctx)
            for col_blk in range(row_blk + 1):
                cols = slice(col_blk * ROWS, (col_blk + 1) * ROWS)
                if dk_sum[col_blk] is None:
                    dk_sum[col_blk] = dk_part[cols]
                    dv_sum[col_blk] = dv_part[cols]
                else:
                    dk_sum[col_blk] = dk_sum[col_blk] + dk_part[cols]
                    dv_sum[col_blk] = dv_sum[col_blk] + dv_part[cols]
        for row_blk in range(n_rows):
            dk_rows[row_blk].append(dk_sum[row_blk].astype(jnp.bfloat16))
            dv_rows[row_blk].append(dv_sum[row_blk].astype(jnp.bfloat16))
    group = pl.program_id(1)
    for kind, rows in enumerate((dq_rows, dk_rows, dv_rows)):
        lane = pl.multiple_of((kind * n_groups + group) * lanes, 128)
        for row_blk in range(n_rows):
            out_ref[0, row_blk * ROWS:(row_blk + 1) * ROWS, pl.ds(lane, lanes)] = jnp.concatenate(rows[row_blk], axis=1)


def attention_calls(n_slots, micro_b, seq_len, width, n_heads):
    head_dim = width // n_heads
    group_heads = next(g for g in range(1, n_heads + 1) if n_heads % g == 0 and (g * head_dim) % 128 == 0)
    lanes = group_heads * head_dim
    n_groups = n_heads // group_heads
    rows = micro_b * seq_len
    flops = micro_b * n_heads * seq_len * seq_len * head_dim * 4

    def qkv_spec(kind):
        return pl.BlockSpec((1, seq_len, lanes), lambda b, g, slot: (slot[0], b, kind * n_groups + g))

    def fwd(slot, qkv_st, ctx_st):
        return pl.pallas_call(
            functools.partial(attn_fwd_kernel, head_dim),
            out_shape=jax.ShapeDtypeStruct((n_slots, rows, width), jnp.bfloat16),
            grid_spec=pltpu.PrefetchScalarGridSpec(
                num_scalar_prefetch=1,
                grid=(micro_b, n_groups),
                in_specs=[qkv_spec(0), qkv_spec(1), qkv_spec(2), pl.BlockSpec(memory_space=pl.ANY)],
                out_specs=pl.BlockSpec((1, seq_len, lanes), lambda b, g, slot: (slot[0], b, g)),
            ),
            input_output_aliases={4: 0},
            cost_estimate=pl.CostEstimate(flops=flops * 6, bytes_accessed=rows * width * 8, transcendentals=0),
            compiler_params=pltpu.CompilerParams(vmem_limit_bytes=32 * 1024 * 1024),
            name='attn_fwd',
        )(slot.reshape(1), qkv_st, qkv_st, qkv_st, ctx_st)

    def bwd(slot, qkv_st, dctx, dqkv_st):
        return pl.pallas_call(
            functools.partial(attn_bwd_kernel, head_dim, n_groups),
            out_shape=jax.ShapeDtypeStruct((n_slots, rows, 3 * width), jnp.bfloat16),
            grid_spec=pltpu.PrefetchScalarGridSpec(
                num_scalar_prefetch=1,
                grid=(micro_b, n_groups),
                in_specs=[qkv_spec(0), qkv_spec(1), qkv_spec(2), pl.BlockSpec((seq_len, lanes), lambda b, g, slot: (b, g)), pl.BlockSpec(memory_space=pl.ANY)],
                out_specs=pl.BlockSpec((1, seq_len, 3 * width), lambda b, g, slot: (slot[0], b, 0)),
            ),
            input_output_aliases={5: 0},
            cost_estimate=pl.CostEstimate(flops=flops * 12, bytes_accessed=rows * width * 14, transcendentals=0),
            compiler_params=pltpu.CompilerParams(vmem_limit_bytes=40 * 1024 * 1024),
            name='attn_bwd',
        )(slot.reshape(1), qkv_st, qkv_st, qkv_st, dctx, dqkv_st)

    return fwd, bwd


def put(stack, value, slot):
    return lax.dynamic_update_index_in_dim(stack, value, slot, 0)


def get(stack, slot):
    return lax.dynamic_index_in_dim(stack, slot, 0, keepdims=False)


def solution(mesh):
    n_stages = mesh.shape['stage']
    n_data = mesh.shape['data']
    act_spec = P(('rep', 'data'))
    weight_spec = P(('rep', 'stage'))
    fast_fwd = [(src, src + 1) for src in range(0, n_stages - 1, 2)]
    slow_fwd = [(src, src + 1) for src in range(1, n_stages - 1, 2)]
    chain_fwd = [(src, src + 1) for src in range(n_stages - 1)]
    fast_bwd = [(dst, src) for src, dst in fast_fwd]
    slow_bwd = [(dst, src) for src, dst in slow_fwd]
    last_delay = (n_stages - 1) + (n_stages - 1) // 2
    swap_pairs = [
        (d * n_stages + s, ((d + 1) % n_data) * n_stages + s) for d in range(n_data) for s in (0, n_stages - 1)
    ]

    def per_device(embeds, targets, w_qkv, w_out, w_up, w_down):
        n_own, micro_b, seq_len, width = embeds.shape
        n_heads = w_qkv.shape[2]
        hidden = w_up.shape[2]
        n_micro = n_own * n_data
        rows = micro_b * seq_len
        w_qkv = w_qkv[0].reshape(3 * width, width)
        w_out = w_out[0].reshape(width, width)
        w_up = w_up[0]
        w_down = w_down[0]
        attn_fwd, attn_bwd = attention_calls(n_micro, micro_b, seq_len, width, n_heads)
        stage_idx = lax.axis_index('stage')
        data_idx = lax.axis_index('data')
        is_first = stage_idx == 0
        is_last = stage_idx == n_stages - 1
        in_by_slow = stage_idx % 2 == 0
        delay = stage_idx + stage_idx // 2
        grad_scale = 1.0 / n_micro
        loss_norm = 1.0 / (n_micro * rows * width)
        n_ticks = n_micro + last_delay
        bf16 = jnp.bfloat16

        def slot_of(turn):
            return lax.rem(turn + data_idx * n_own, n_micro)

        own = jnp.where(is_last, targets, embeds).reshape(n_own, rows, width)
        (ext, a_st, n1_st, qkv_st, ctx_st, h_st, n2_st, pre_st, u_st, g_st, dpre_st, dh_st, dqkv_st, dx_st) = empty_arrays(
            ((n_micro, rows, width), bf16),
            ((n_micro, rows, width), bf16),
            ((n_micro, rows, width), bf16),
            ((n_micro, rows, 3 * width), bf16),
            ((n_micro, rows, width), bf16),
            ((n_micro, rows, width), bf16),
            ((n_micro, rows, width), bf16),
            ((n_micro, rows, hidden), jnp.float32),
            ((n_micro, rows, hidden), bf16),
            ((n_micro, rows, width), bf16),
            ((n_micro, rows, hidden), bf16),
            ((n_micro, rows, width), bf16),
            ((n_micro, rows, 3 * width), bf16),
            ((n_own + 1, rows, width), bf16),
        )
        ext = lax.dynamic_update_slice(ext, own, (0, 0, 0))
        micro_zeros = jnp.zeros((rows, width), bf16)

        def fwd_tick(tick, carry):
            cur_in, prev_out, ext, a_st, n1_st, qkv_st, ctx_st, h_st, n2_st, pre_st, u_st, g_st, losses = carry
            swap_idx = jnp.minimum(tick, n_own - 1)
            swapped = lax.ppermute(get(ext, swap_idx), ('data', 'stage'), swap_pairs)
            slow_in = lax.ppermute(prev_out, 'stage', slow_fwd)
            turn = jnp.clip(tick - delay, 0, n_micro - 1)
            slot = slot_of(turn)
            outside = lax.optimization_barrier(get(ext, turn))
            act_in = jnp.where(is_first, outside, cur_in)
            a_st = put(a_st, act_in, slot)
            act32 = act_in.astype(jnp.float32)
            normed1 = rms_norm(act32).astype(bf16)
            n1_st = put(n1_st, normed1, slot)
            qkv_st = put(qkv_st, dot_nt(normed1, w_qkv).astype(bf16), slot)
            ctx_st = attn_fwd(slot, qkv_st, ctx_st)
            hidden16 = (act32 + dot_nn(get(ctx_st, slot), w_out)).astype(bf16)
            h_st = put(h_st, hidden16, slot)
            hidden32 = hidden16.astype(jnp.float32)
            normed2 = rms_norm(hidden32).astype(bf16)
            n2_st = put(n2_st, normed2, slot)
            pre_act = dot_nn(normed2, w_up)
            pre_st = put(pre_st, pre_act, slot)
            u_st = lax.optimization_barrier(put(u_st, gelu_tanh(pre_act).astype(bf16), slot))
            act_out = (hidden32 + dot_nn(get(u_st, slot), w_down)).astype(bf16)
            error = act_out.astype(jnp.float32) - outside.astype(jnp.float32)
            losses = put(losses, 0.5 * jnp.sum(error * error) * loss_norm, slot)
            g_st = put(g_st, (error * grad_scale).astype(bf16), slot)
            fast_in = lax.ppermute(act_out, 'stage', fast_fwd)
            hold = tick - delay >= n_micro - 1
            cur_in = jnp.where(hold, cur_in, jnp.where(in_by_slow, slow_in, fast_in))
            swapped = lax.optimization_barrier((swapped, act_out))[0]
            ext = put(ext, swapped, n_own + swap_idx)
            return cur_in, act_out, ext, a_st, n1_st, qkv_st, ctx_st, h_st, n2_st, pre_st, u_st, g_st, losses

        carry = (micro_zeros, micro_zeros, ext, a_st, n1_st, qkv_st, ctx_st, h_st, n2_st, pre_st, u_st, g_st, jnp.zeros((n_micro,), jnp.float32))
        carry = lax.fori_loop(0, n_ticks, fwd_tick, carry)
        _, _, _, a_st, n1_st, qkv_st, ctx_st, h_st, n2_st, pre_st, u_st, g_st, losses = carry

        def bwd_tick(tick, carry):
            cur_in, prev_out, chain, g_st, dpre_st, dh_st, dqkv_st, dx_st = carry
            chained = lax.ppermute(chain, 'stage', chain_fwd)
            slow_in = lax.ppermute(prev_out, 'stage', slow_bwd)
            from_last = tick - (last_delay - delay)
            slot = slot_of(jnp.clip(from_last, 0, n_micro - 1))
            grad_out = jnp.where(is_last, get(g_st, slot), cur_in)
            g_st = put(g_st, grad_out, slot)
            d_upper = dot_nt(grad_out, w_down)
            d_pre = jax.vjp(gelu_tanh, get(pre_st, slot))[1](d_upper)[0].astype(bf16)
            dpre_st = put(dpre_st, d_pre, slot)
            d_normed2 = dot_nt(d_pre, w_up)
            hidden32 = get(h_st, slot).astype(jnp.float32)
            d_hidden = grad_out.astype(jnp.float32) + jax.vjp(rms_norm, hidden32)[1](d_normed2)[0]
            d_hidden16 = d_hidden.astype(bf16)
            dh_st = put(dh_st, d_hidden16, slot)
            d_context = dot_nt(d_hidden16, w_out).astype(bf16)
            dqkv_st = attn_bwd(slot, qkv_st, d_context, dqkv_st)
            d_normed1 = dot_nn(get(dqkv_st, slot), w_qkv)
            act32 = get(a_st, slot).astype(jnp.float32)
            grad_in = (d_hidden + jax.vjp(rms_norm, act32)[1](d_normed1)[0]).astype(bf16)
            fast_in = lax.ppermute(grad_in, 'stage', fast_bwd)
            hold = from_last >= n_micro - 1
            cur_in = jnp.where(hold, cur_in, jnp.where(in_by_slow, fast_in, slow_in))
            chain = jnp.where(is_first, grad_in, chained)
            own_idx = tick - last_delay - stage_idx
            dx_st = put(dx_st, chain, jnp.where((own_idx >= 0) & (own_idx < n_own), own_idx, n_own))
            return cur_in, grad_in, chain, g_st, dpre_st, dh_st, dqkv_st, dx_st

        carry = (micro_zeros, micro_zeros, micro_zeros, g_st, dpre_st, dh_st, dqkv_st, dx_st)
        carry = lax.fori_loop(0, n_ticks, bwd_tick, carry)
        _, _, _, g_st, dpre_st, dh_st, dqkv_st, dx_st = carry

        def weight_grad(lhs_st, rhs_st):
            return lax.optimization_barrier(dot_tn(lhs_st.reshape(n_micro * rows, -1), rhs_st.reshape(n_micro * rows, -1)))

        d_qkv = weight_grad(dqkv_st, n1_st).reshape(1, 3, n_heads, width // n_heads, width)
        d_out = weight_grad(ctx_st, dh_st).reshape(1, n_heads, width // n_heads, width)
        d_up = weight_grad(n2_st, dpre_st)[None]
        d_down = weight_grad(u_st, g_st)[None]
        loss = lax.psum(jnp.where(is_last, jnp.sum(losses), 0.0), 'stage').reshape(1)
        d_embeds = dx_st[:n_own].reshape(n_own, micro_b, seq_len, width)
        return loss, d_qkv, d_out, d_up, d_down, d_embeds

    return jax.shard_map(per_device, mesh=mesh, in_specs=(act_spec, act_spec, weight_spec, weight_spec, weight_spec, weight_spec), out_specs=(P('rep'), weight_spec, weight_spec, weight_spec, weight_spec, act_spec), check_vma=False)
```

time: 7320 us -> 4270 us (0.58)
  waiting for transfers between devices: 2590 us -> 82.4 us
  other arithmetic: 1480 us -> 442 us
  Pallas kernels: 0 us -> 992 us
  starting transfers between devices: 1170 us -> 187 us
  matrix products: 1490 us -> 2160 us
  local copies, waits for them, and re-layouts: 472 us -> 358 us
    psum x2 -> x0, waiting for transfers between devices: 2590 us -> none  [the longest x1 2450 us: per_device(): d_weights = tuple((lax.psum(total, 'data')[None] for total in grad_sums))]
    add x44 -> x0, other arithmetic: 1140 us -> none  [the longest x40 1130 us: tick_body(): total + piece]
    pallas_call x0 -> x25, Pallas kernels: none -> 992 us  [the longest x12 595 us: bwd(): pl.pallas_call(functools.partial(attn_bwd_kernel, head_dim, n_groups), ou...]
    ppermute x20 -> x72, starting transfers between devices: 1170 us -> 187 us  [the longest x12 47.7 us: fwd_tick(): fast_in = lax.ppermute(act_out, 'stage', fast_fwd)]
    dot_general x88 -> x100, matrix products: 1490 us -> 2160 us  [the longest x48 913 us: dot_nt(): lax.dot_general(lhs, rhs, (((1,), (1,)), ((), ())), preferred_element_typ...]
    another operation x46 -> x1, local copies, waits for them, and re-layouts: 306 us -> 0.51 us
    dynamic_update_slice x0 -> x37, local copies, waits for them, and re-layouts: none -> 201 us  [the longest x36 193 us: put(): return lax.dynamic_update_index_in_dim(stack, value, slot, 0)]
    sub x8 -> x0, other arithmetic: 184 us -> none  [layer_forward(): probs32 = jax.nn.softmax(jnp.where(causal, scores, -1e+30), axis=-1)]
  transfers between devices with their start and end apart: 22 -> 72, of which waited for: 2 -> 12; matrix products, arithmetic and copies ran while one was open for 16% -> 55% of each run, Pallas kernels for 0% -> 23%
where the time goes in v1:
time: 4270 us; the launch traced here: 4260 us
  matrix products  2160 us (51%)
  Pallas kernels  992 us (23%)
  other arithmetic  442 us (10%)
  local copies, waits for them, and re-layouts  358 us (8%)
  starting transfers between devices  187 us (4%)
  waiting for transfers between devices  82.4 us (2%)
    dot_general x48, matrix products, dot_nt(): lax.dot_general(lhs, rhs, (((1,), (1,)), ((), ())), preferred_element_typ...  913 us
    dot_general x48, matrix products, dot_nn(): lax.dot_general(lhs, rhs, (((1,), (0,)), ((), ())), preferred_element_typ...  850 us
    pallas_call x12, Pallas kernels, bwd(): pl.pallas_call(functools.partial(attn_bwd_kernel, head_dim, n_groups), ou...  595 us
    dot_general x4, matrix products, dot_tn(): lax.dot_general(lhs, rhs, (((0,), (0,)), ((), ())), preferred_element_typ...  401 us
    pallas_call x12, Pallas kernels, fwd(): pl.pallas_call(functools.partial(attn_fwd_kernel, head_dim), out_shape=ja...  397 us
    dynamic_update_slice x48, other arithmetic, put(): return lax.dynamic_update_index_in_dim(stack, value, slot, 0)  197 us
    dynamic_update_slice x36, local copies, waits for them, and re-layouts, put(): return lax.dynamic_update_index_in_dim(stack, value, slot, 0)  193 us
    while x228, local copies, waits for them, and re-layouts  98.8 us
  transfers between devices with their start and end apart: 72, of which 12 were waited for; matrix products, arithmetic and copies ran while one was open for 55% of the time, Pallas kernels for 23%

profile of v1, /device:TPU:0, one launch (start us, length us, event | category | flops | bytes accessed | tf_op | source)
XLA Modules:
  0.0 4262.2 jit_solution(2812851024993825859)
XLA Ops:
  18.3 1853.0 %while.70 = (s32[]{:T(128)}, bf16[768,1536]{1,0:T(8,128)(2,1)}, bf16[768,1536]{1,0:T(8,128)(2,1)}, bf16[8,768,1536]{2,1,0:T(8,128)(2,1)}, bf16[8,768,1536]{2,1,0...) while((s32[]{:T(128)}, bf16[768,1536]{1,0:T(8,128)(2,1)}, ...), condition=%wide.region_4.5_spmd.clone, body=%wide.region_0.4_spmd.clone.sunk | while | flops 54451372032 | bytes 287867392 | solution.py:262
  46.9 33.1 attn_fwd.8
  87.1 24.9 bitcast_dynamic-update-slice_fusion.20
  111.9 22.3 fusion.102
  199.0 33.1 attn_fwd.8
  239.2 24.7 bitcast_dynamic-update-slice_fusion.20
  354.1 33.0 attn_fwd.8
  394.3 24.9 bitcast_dynamic-update-slice_fusion.20
  419.2 22.3 fusion.102
  507.6 33.0 attn_fwd.8
  547.8 24.8 bitcast_dynamic-update-slice_fusion.20
  660.0 33.1 attn_fwd.8
  700.3 24.8 bitcast_dynamic-update-slice_fusion.20
  725.0 22.3 fusion.102
  813.6 33.1 attn_fwd.8
  853.8 24.8 bitcast_dynamic-update-slice_fusion.20
  878.6 22.4 fusion.102
  966.6 33.0 attn_fwd.8
  1006.8 24.8 bitcast_dynamic-update-slice_fusion.20
  1031.6 22.3 fusion.102
  1119.6 33.0 attn_fwd.8
  1159.8 24.9 bitcast_dynamic-update-slice_fusion.20
  1184.7 22.3 fusion.102
  1273.0 33.0 attn_fwd.8
  1313.2 24.9 bitcast_dynamic-update-slice_fusion.20
  1338.1 22.3 fusion.102
  1425.6 33.0 attn_fwd.8
  1465.8 24.9 bitcast_dynamic-update-slice_fusion.20
  1490.6 22.3 fusion.102
  1578.8 33.0 attn_fwd.8
  1619.0 24.9 bitcast_dynamic-update-slice_fusion.20
  1643.9 22.3 fusion.102
  1731.7 33.0 attn_fwd.8
  1771.9 24.9 bitcast_dynamic-update-slice_fusion.20
  1796.8 22.3 fusion.102
  1871.4 1968.6 %while.71 = (s32[]{:T(128)}, bf16[768,1536]{1,0:T(8,128)(2,1)}, bf16[768,1536]{1,0:T(8,128)(2,1)}, bf16[768,1536]{1,0:T(8,128)(2,1)}, bf16[8,768,1536]{2,1,0:T(8...) while((s32[]{:T(128)}, bf16[768,1536]{1,0:T(8,128)(2,1)}, ...), condition=%wide.region_12.13_spmd.clone, body=%wide.region_7.12_spmd.clone.sunk | while | flops 65365479424 | bytes 302041280 | solution.py:295
  1882.9 31.8 bitcast_dynamic-update-slice_fusion.24
  1949.0 49.6 %attn_bwd.8 = bf16[8,768,4608]{2,1,0:T(8,128)(2,1)} custom-call(s32[1]{0:T(128)} %bitcast.177.slot_ref, bf16[8,768,4608]{2,1,0:T(8,128)(2,1)} %get-tuple-element.1864.q_ref.k_ref.v_ref, bf16[8,768,4608]{2,1,0:T(8,128)(2,1)} %get-tuple-element.1864.q_ref.k_ref.v_ref, ...), custom_call_target="tpu_custom_call", output_to_operand_aliasing={{}: (5, {})} | custom-call | flops 21743271936 | bytes 16515072 | tf_op jit(solution)/shard_map/while/body/eval_jaxpr/attn_bwd/pallas_call | solution.py:141
  2045.8 31.8 bitcast_dynamic-update-slice_fusion.24
  2111.9 49.6 %attn_bwd.8 = bf16[8,768,4608]{2,1,0:T(8,128)(2,1)} custom-call(s32[1]{0:T(128)} %bitcast.177.slot_ref, bf16[8,768,4608]{2,1,0:T(8,128)(2,1)} %get-tuple-element.1864.q_ref.k_ref.v_ref, bf16[8,768,4608]{2,1,0:T(8,128)(2,1)} %get-tuple-element.1864.q_ref.k_ref.v_ref, ...), custom_call_target="tpu_custom_call", output_to_operand_aliasing={{}: (5, {})} | custom-call | flops 21743271936 | bytes 16515072 | tf_op jit(solution)/shard_map/while/body/eval_jaxpr/attn_bwd/pallas_call | solution.py:141
  2208.7 31.8 bitcast_dynamic-update-slice_fusion.24
  2274.8 49.6 %attn_bwd.8 = bf16[8,768,4608]{2,1,0:T(8,128)(2,1)} custom-call(s32[1]{0:T(128)} %bitcast.177.slot_ref, bf16[8,768,4608]{2,1,0:T(8,128)(2,1)} %get-tuple-element.1864.q_ref.k_ref.v_ref, bf16[8,768,4608]{2,1,0:T(8,128)(2,1)} %get-tuple-element.1864.q_ref.k_ref.v_ref, ...), custom_call_target="tpu_custom_call", output_to_operand_aliasing={{}: (5, {})} | custom-call | flops 21743271936 | bytes 16515072 | tf_op jit(solution)/shard_map/while/body/eval_jaxpr/attn_bwd/pallas_call | solution.py:141
  2372.6 31.8 bitcast_dynamic-update-slice_fusion.24
  2438.7 49.6 %attn_bwd.8 = bf16[8,768,4608]{2,1,0:T(8,128)(2,1)} custom-call(s32[1]{0:T(128)} %bitcast.177.slot_ref, bf16[8,768,4608]{2,1,0:T(8,128)(2,1)} %get-tuple-element.1864.q_ref.k_ref.v_ref, bf16[8,768,4608]{2,1,0:T(8,128)(2,1)} %get-tuple-element.1864.q_ref.k_ref.v_ref, ...), custom_call_target="tpu_custom_call", output_to_operand_aliasing={{}: (5, {})} | custom-call | flops 21743271936 | bytes 16515072 | tf_op jit(solution)/shard_map/while/body/eval_jaxpr/attn_bwd/pallas_call | solution.py:141
  2537.3 31.8 bitcast_dynamic-update-slice_fusion.24
  2603.3 49.6 %attn_bwd.8 = bf16[8,768,4608]{2,1,0:T(8,128)(2,1)} custom-call(s32[1]{0:T(128)} %bitcast.177.slot_ref, bf16[8,768,4608]{2,1,0:T(8,128)(2,1)} %get-tuple-element.1864.q_ref.k_ref.v_ref, bf16[8,768,4608]{2,1,0:T(8,128)(2,1)} %get-tuple-element.1864.q_ref.k_ref.v_ref, ...), custom_call_target="tpu_custom_call", output_to_operand_aliasing={{}: (5, {})} | custom-call | flops 21743271936 | bytes 16515072 | tf_op jit(solution)/shard_map/while/body/eval_jaxpr/attn_bwd/pallas_call | solution.py:141
  2701.9 31.8 bitcast_dynamic-update-slice_fusion.24
  2767.8 49.7 %attn_bwd.8 = bf16[8,768,4608]{2,1,0:T(8,128)(2,1)} custom-call(s32[1]{0:T(128)} %bitcast.177.slot_ref, bf16[8,768,4608]{2,1,0:T(8,128)(2,1)} %get-tuple-element.1864.q_ref.k_ref.v_ref, bf16[8,768,4608]{2,1,0:T(8,128)(2,1)} %get-tuple-element.1864.q_ref.k_ref.v_ref, ...), custom_call_target="tpu_custom_call", output_to_operand_aliasing={{}: (5, {})} | custom-call | flops 21743271936 | bytes 16515072 | tf_op jit(solution)/shard_map/while/body/eval_jaxpr/attn_bwd/pallas_call | solution.py:141
  2866.5 31.8 bitcast_dynamic-update-slice_fusion.24
  2932.5 49.7 %attn_bwd.8 = bf16[8,768,4608]{2,1,0:T(8,128)(2,1)} custom-call(s32[1]{0:T(128)} %bitcast.177.slot_ref, bf16[8,768,4608]{2,1,0:T(8,128)(2,1)} %get-tuple-element.1864.q_ref.k_ref.v_ref, bf16[8,768,4608]{2,1,0:T(8,128)(2,1)} %get-tuple-element.1864.q_ref.k_ref.v_ref, ...), custom_call_target="tpu_custom_call", output_to_operand_aliasing={{}: (5, {})} | custom-call | flops 21743271936 | bytes 16515072 | tf_op jit(solution)/shard_map/while/body/eval_jaxpr/attn_bwd/pallas_call | solution.py:141
  3031.0 31.8 bitcast_dynamic-update-slice_fusion.24
  3097.0 49.6 %attn_bwd.8 = bf16[8,768,4608]{2,1,0:T(8,128)(2,1)} custom-call(s32[1]{0:T(128)} %bitcast.177.slot_ref, bf16[8,768,4608]{2,1,0:T(8,128)(2,1)} %get-tuple-element.1864.q_ref.k_ref.v_ref, bf16[8,768,4608]{2,1,0:T(8,128)(2,1)} %get-tuple-element.1864.q_ref.k_ref.v_ref, ...), custom_call_target="tpu_custom_call", output_to_operand_aliasing={{}: (5, {})} | custom-call | flops 21743271936 | bytes 16515072 | tf_op jit(solution)/shard_map/while/body/eval_jaxpr/attn_bwd/pallas_call | solution.py:141
  3195.7 31.9 bitcast_dynamic-update-slice_fusion.24
  3261.7 49.6 %attn_bwd.8 = bf16[8,768,4608]{2,1,0:T(8,128)(2,1)} custom-call(s32[1]{0:T(128)} %bitcast.177.slot_ref, bf16[8,768,4608]{2,1,0:T(8,128)(2,1)} %get-tuple-element.1864.q_ref.k_ref.v_ref, bf16[8,768,4608]{2,1,0:T(8,128)(2,1)} %get-tuple-element.1864.q_ref.k_ref.v_ref, ...), custom_call_target="tpu_custom_call", output_to_operand_aliasing={{}: (5, {})} | custom-call | flops 21743271936 | bytes 16515072 | tf_op jit(solution)/shard_map/while/body/eval_jaxpr/attn_bwd/pallas_call | solution.py:141
  3360.4 31.8 bitcast_dynamic-update-slice_fusion.24
  3426.4 49.6 %attn_bwd.8 = bf16[8,768,4608]{2,1,0:T(8,128)(2,1)} custom-call(s32[1]{0:T(128)} %bitcast.177.slot_ref, bf16[8,768,4608]{2,1,0:T(8,128)(2,1)} %get-tuple-element.1864.q_ref.k_ref.v_ref, bf16[8,768,4608]{2,1,0:T(8,128)(2,1)} %get-tuple-element.1864.q_ref.k_ref.v_ref, ...), custom_call_target="tpu_custom_call", output_to_operand_aliasing={{}: (5, {})} | custom-call | flops 21743271936 | bytes 16515072 | tf_op jit(solution)/shard_map/while/body/eval_jaxpr/attn_bwd/pallas_call | solution.py:141
  3525.2 31.9 bitcast_dynamic-update-slice_fusion.24
  3591.3 49.6 %attn_bwd.8 = bf16[8,768,4608]{2,1,0:T(8,128)(2,1)} custom-call(s32[1]{0:T(128)} %bitcast.177.slot_ref, bf16[8,768,4608]{2,1,0:T(8,128)(2,1)} %get-tuple-element.1864.q_ref.k_ref.v_ref, bf16[8,768,4608]{2,1,0:T(8,128)(2,1)} %get-tuple-element.1864.q_ref.k_ref.v_ref, ...), custom_call_target="tpu_custom_call", output_to_operand_aliasing={{}: (5, {})} | custom-call | flops 21743271936 | bytes 16515072 | tf_op jit(solution)/shard_map/while/body/eval_jaxpr/attn_bwd/pallas_call | solution.py:141
  3689.7 31.8 bitcast_dynamic-update-slice_fusion.24
  3755.6 49.7 %attn_bwd.8 = bf16[8,768,4608]{2,1,0:T(8,128)(2,1)} custom-call(s32[1]{0:T(128)} %bitcast.177.slot_ref, bf16[8,768,4608]{2,1,0:T(8,128)(2,1)} %get-tuple-element.1864.q_ref.k_ref.v_ref, bf16[8,768,4608]{2,1,0:T(8,128)(2,1)} %get-tuple-element.1864.q_ref.k_ref.v_ref, ...), custom_call_target="tpu_custom_call", output_to_operand_aliasing={{}: (5, {})} | custom-call | flops 21743271936 | bytes 16515072 | tf_op jit(solution)/shard_map/while/body/eval_jaxpr/attn_bwd/pallas_call | solution.py:141
  3840.0 130.6 %convolution_bitcast_fusion = f32[6144,1536]{1,0:T(8,128)} fusion(bf16[8,768,6144]{2,1,0:T(8,128)(2,1)} %get-tuple-element.1094, bf16[8,768,1536]{2,1,0:T(8,128)(2,1)} %get-tuple-element.1095), kind=kOutput, calls=%fused_computation.101 | convolution fusion | flops 115964116992 | bytes 132120576 | tf_op jit(solution)/shard_map/dot_general | solution.py:32
  3970.6 132.8 %convolution_bitcast_fusion.1 = f32[1536,6144]{1,0:T(8,128)} fusion(bf16[8,768,1536]{2,1,0:T(8,128)(2,1)} %get-tuple-element.1092, bf16[8,768,6144]{2,1,0:T(8,128)(2,1)} %get-tuple-element.1093), kind=kOutput, calls=%fused_computation.102 | convolution fusion | flops 115964116992 | bytes 132120576 | tf_op jit(solution)/shard_map/dot_general | solution.py:32
  4103.4 37.8 convolution_bitcast_fusion.3
  4141.2 100.1 %convolution_bitcast_fusion.2 = f32[4608,1536]{1,0:T(8,128)} fusion(bf16[8,768,4608]{2,1,0:T(8,128)(2,1)} %get-tuple-element.1088, bf16[8,768,1536]{2,1,0:T(8,128)(2,1)} %get-tuple-element.1089), kind=kOutput, calls=%fused_computation.103 | convolution fusion | flops 86973087744 | bytes 103809024 | tf_op jit(solution)/shard_map/dot_general | solution.py:32
  (688 shorter events, 1940.0 us)
Async XLA Ops:
  22.4 141.9 %collective-permute-start.2 = (bf16[768,1536]{1,0:T(8,128)(2,1)}, bf16[768,1536]{1,0:T(8,128)(2,1)}, u32[]{:S(2)}, u32[]{:S(2)}) collective-permute-start(bf16[768,1536]{1,0:T(8,128)(2,1)} %get-tuple-element.1647), channel_id=1, source_target_pairs={{0,4},{3,7},{4,0},{7,3}} | collective-permute-start | bytes 7077896 | tf_op jit(solution)/shard_map/while/body/eval_jaxpr/ppermute | solution.py:230
  134.2 33.3 collective-permute-start.1
  138.5 29.0 collective-permute-start
  175.7 144.0 %collective-permute-start.2 = (bf16[768,1536]{1,0:T(8,128)(2,1)}, bf16[768,1536]{1,0:T(8,128)(2,1)}, u32[]{:S(2)}, u32[]{:S(2)}) collective-permute-start(bf16[768,1536]{1,0:T(8,128)(2,1)} %get-tuple-element.1647), channel_id=1, source_target_pairs={{0,4},{3,7},{4,0},{7,3}} | collective-permute-start | bytes 7077896 | tf_op jit(solution)/shard_map/while/body/eval_jaxpr/ppermute | solution.py:230
  286.3 36.6 collective-permute-start.1
  293.8 29.0 collective-permute-start
  331.0 141.5 %collective-permute-start.2 = (bf16[768,1536]{1,0:T(8,128)(2,1)}, bf16[768,1536]{1,0:T(8,128)(2,1)}, u32[]{:S(2)}, u32[]{:S(2)}) collective-permute-start(bf16[768,1536]{1,0:T(8,128)(2,1)} %get-tuple-element.1647), channel_id=1, source_target_pairs={{0,4},{3,7},{4,0},{7,3}} | collective-permute-start | bytes 7077896 | tf_op jit(solution)/shard_map/while/body/eval_jaxpr/ppermute | solution.py:230
  441.5 34.3 collective-permute-start.1
  446.9 28.9 collective-permute-start
  483.9 141.9 %collective-permute-start.2 = (bf16[768,1536]{1,0:T(8,128)(2,1)}, bf16[768,1536]{1,0:T(8,128)(2,1)}, u32[]{:S(2)}, u32[]{:S(2)}) collective-permute-start(bf16[768,1536]{1,0:T(8,128)(2,1)} %get-tuple-element.1647), channel_id=1, source_target_pairs={{0,4},{3,7},{4,0},{7,3}} | collective-permute-start | bytes 7077896 | tf_op jit(solution)/shard_map/while/body/eval_jaxpr/ppermute | solution.py:230
  594.8 34.2 collective-permute-start.1
  600.2 28.9 collective-permute-start
  637.2 141.8 %collective-permute-start.2 = (bf16[768,1536]{1,0:T(8,128)(2,1)}, bf16[768,1536]{1,0:T(8,128)(2,1)}, u32[]{:S(2)}, u32[]{:S(2)}) collective-permute-start(bf16[768,1536]{1,0:T(8,128)(2,1)} %get-tuple-element.1647), channel_id=1, source_target_pairs={{0,4},{3,7},{4,0},{7,3}} | collective-permute-start | bytes 7077896 | tf_op jit(solution)/shard_map/while/body/eval_jaxpr/ppermute | solution.py:230
  747.3 34.9 collective-permute-start.1
  753.1 29.1 collective-permute-start
  790.4 141.4 %collective-permute-start.2 = (bf16[768,1536]{1,0:T(8,128)(2,1)}, bf16[768,1536]{1,0:T(8,128)(2,1)}, u32[]{:S(2)}, u32[]{:S(2)}) collective-permute-start(bf16[768,1536]{1,0:T(8,128)(2,1)} %get-tuple-element.1647), channel_id=1, source_target_pairs={{0,4},{3,7},{4,0},{7,3}} | collective-permute-start | bytes 7077896 | tf_op jit(solution)/shard_map/while/body/eval_jaxpr/ppermute | solution.py:230
  901.0 34.0 collective-permute-start.1
  906.0 29.0 collective-permute-start
  943.1 142.4 %collective-permute-start.2 = (bf16[768,1536]{1,0:T(8,128)(2,1)}, bf16[768,1536]{1,0:T(8,128)(2,1)}, u32[]{:S(2)}, u32[]{:S(2)}) collective-permute-start(bf16[768,1536]{1,0:T(8,128)(2,1)} %get-tuple-element.1647), channel_id=1, source_target_pairs={{0,4},{3,7},{4,0},{7,3}} | collective-permute-start | bytes 7077896 | tf_op jit(solution)/shard_map/while/body/eval_jaxpr/ppermute | solution.py:230
  1053.9 34.8 collective-permute-start.1
  1059.6 29.1 collective-permute-start
  1096.9 141.1 %collective-permute-start.2 = (bf16[768,1536]{1,0:T(8,128)(2,1)}, bf16[768,1536]{1,0:T(8,128)(2,1)}, u32[]{:S(2)}, u32[]{:S(2)}) collective-permute-start(bf16[768,1536]{1,0:T(8,128)(2,1)} %get-tuple-element.1647), channel_id=1, source_target_pairs={{0,4},{3,7},{4,0},{7,3}} | collective-permute-start | bytes 7077896 | tf_op jit(solution)/shard_map/while/body/eval_jaxpr/ppermute | solution.py:230
  1207.0 34.3 collective-permute-start.1
  1212.4 28.9 collective-permute-start
  1249.4 141.8 %collective-permute-start.2 = (bf16[768,1536]{1,0:T(8,128)(2,1)}, bf16[768,1536]{1,0:T(8,128)(2,1)}, u32[]{:S(2)}, u32[]{:S(2)}) collective-permute-start(bf16[768,1536]{1,0:T(8,128)(2,1)} %get-tuple-element.1647), channel_id=1, source_target_pairs={{0,4},{3,7},{4,0},{7,3}} | collective-permute-start | bytes 7077896 | tf_op jit(solution)/shard_map/while/body/eval_jaxpr/ppermute | solution.py:230
  1360.4 34.1 collective-permute-start.1
  1365.6 28.9 collective-permute-start
  1402.6 141.6 %collective-permute-start.2 = (bf16[768,1536]{1,0:T(8,128)(2,1)}, bf16[768,1536]{1,0:T(8,128)(2,1)}, u32[]{:S(2)}, u32[]{:S(2)}) collective-permute-start(bf16[768,1536]{1,0:T(8,128)(2,1)} %get-tuple-element.1647), channel_id=1, source_target_pairs={{0,4},{3,7},{4,0},{7,3}} | collective-permute-start | bytes 7077896 | tf_op jit(solution)/shard_map/while/body/eval_jaxpr/ppermute | solution.py:230
  1512.9 34.5 collective-permute-start.1
  1518.6 28.9 collective-permute-start
  1555.6 141.7 %collective-permute-start.2 = (bf16[768,1536]{1,0:T(8,128)(2,1)}, bf16[768,1536]{1,0:T(8,128)(2,1)}, u32[]{:S(2)}, u32[]{:S(2)}) collective-permute-start(bf16[768,1536]{1,0:T(8,128)(2,1)} %get-tuple-element.1647), channel_id=1, source_target_pairs={{0,4},{3,7},{4,0},{7,3}} | collective-permute-start | bytes 7077896 | tf_op jit(solution)/shard_map/while/body/eval_jaxpr/ppermute | solution.py:230
  1666.2 34.3 collective-permute-start.1
  1671.6 28.9 collective-permute-start
  1708.6 141.7 %collective-permute-start.2 = (bf16[768,1536]{1,0:T(8,128)(2,1)}, bf16[768,1536]{1,0:T(8,128)(2,1)}, u32[]{:S(2)}, u32[]{:S(2)}) collective-permute-start(bf16[768,1536]{1,0:T(8,128)(2,1)} %get-tuple-element.1647), channel_id=1, source_target_pairs={{0,4},{3,7},{4,0},{7,3}} | collective-permute-start | bytes 7077896 | tf_op jit(solution)/shard_map/while/body/eval_jaxpr/ppermute | solution.py:230
  1819.1 34.4 collective-permute-start.1
  1824.7 28.9 collective-permute-start
  1873.0 142.2 %collective-permute-start.3 = (bf16[768,1536]{1,0:T(8,128)(2,1)}, bf16[768,1536]{1,0:T(8,128)(2,1)}, u32[]{:S(2)}, u32[]{:S(2)}) collective-permute-start(bf16[768,1536]{1,0:T(8,128)(2,1)} %broadcast_select_fusion.14), channel_id=1, source_target_pairs={{0,1},{1,2},{2,3},{4,5},{5,6},{6,7}} | collective-permute-start | bytes 7077896 | tf_op jit(solution)/shard_map/while/body/eval_jaxpr/ppermute | solution.py:267
  1878.9 142.8 %collective-permute-start.5 = (bf16[768,1536]{1,0:T(8,128)(2,1)}, bf16[768,1536]{1,0:T(8,128)(2,1)}, u32[]{:S(2)}, u32[]{:S(2)}) collective-permute-start(bf16[768,1536]{1,0:T(8,128)(2,1)} %broadcast_select_fusion.15), channel_id=1, source_target_pairs={{2,1},{6,5}} | collective-permute-start | bytes 7077896 | tf_op jit(solution)/shard_map/while/body/eval_jaxpr/ppermute | solution.py:268
  2034.3 143.7 %collective-permute-start.3 = (bf16[768,1536]{1,0:T(8,128)(2,1)}, bf16[768,1536]{1,0:T(8,128)(2,1)}, u32[]{:S(2)}, u32[]{:S(2)}) collective-permute-start(bf16[768,1536]{1,0:T(8,128)(2,1)} %broadcast_select_fusion.14), channel_id=1, source_target_pairs={{0,1},{1,2},{2,3},{4,5},{5,6},{6,7}} | collective-permute-start | bytes 7077896 | tf_op jit(solution)/shard_map/while/body/eval_jaxpr/ppermute | solution.py:267
  2041.1 143.5 %collective-permute-start.5 = (bf16[768,1536]{1,0:T(8,128)(2,1)}, bf16[768,1536]{1,0:T(8,128)(2,1)}, u32[]{:S(2)}, u32[]{:S(2)}) collective-permute-start(bf16[768,1536]{1,0:T(8,128)(2,1)} %broadcast_select_fusion.15), channel_id=1, source_target_pairs={{2,1},{6,5}} | collective-permute-start | bytes 7077896 | tf_op jit(solution)/shard_map/while/body/eval_jaxpr/ppermute | solution.py:268
  2197.3 143.7 %collective-permute-start.3 = (bf16[768,1536]{1,0:T(8,128)(2,1)}, bf16[768,1536]{1,0:T(8,128)(2,1)}, u32[]{:S(2)}, u32[]{:S(2)}) collective-permute-start(bf16[768,1536]{1,0:T(8,128)(2,1)} %broadcast_select_fusion.14), channel_id=1, source_target_pairs={{0,1},{1,2},{2,3},{4,5},{5,6},{6,7}} | collective-permute-start | bytes 7077896 | tf_op jit(solution)/shard_map/while/body/eval_jaxpr/ppermute | solution.py:267
  2204.0 143.5 %collective-permute-start.5 = (bf16[768,1536]{1,0:T(8,128)(2,1)}, bf16[768,1536]{1,0:T(8,128)(2,1)}, u32[]{:S(2)}, u32[]{:S(2)}) collective-permute-start(bf16[768,1536]{1,0:T(8,128)(2,1)} %broadcast_select_fusion.15), channel_id=1, source_target_pairs={{2,1},{6,5}} | collective-permute-start | bytes 7077896 | tf_op jit(solution)/shard_map/while/body/eval_jaxpr/ppermute | solution.py:268
  2361.1 143.7 %collective-permute-start.3 = (bf16[768,1536]{1,0:T(8,128)(2,1)}, bf16[768,1536]{1,0:T(8,128)(2,1)}, u32[]{:S(2)}, u32[]{:S(2)}) collective-permute-start(bf16[768,1536]{1,0:T(8,128)(2,1)} %broadcast_select_fusion.14), channel_id=1, source_target_pairs={{0,1},{1,2},{2,3},{4,5},{5,6},{6,7}} | collective-permute-start | bytes 7077896 | tf_op jit(solution)/shard_map/while/body/eval_jaxpr/ppermute | solution.py:267
  2367.9 143.5 %collective-permute-start.5 = (bf16[768,1536]{1,0:T(8,128)(2,1)}, bf16[768,1536]{1,0:T(8,128)(2,1)}, u32[]{:S(2)}, u32[]{:S(2)}) collective-permute-start(bf16[768,1536]{1,0:T(8,128)(2,1)} %broadcast_select_fusion.15), channel_id=1, source_target_pairs={{2,1},{6,5}} | collective-permute-start | bytes 7077896 | tf_op jit(solution)/shard_map/while/body/eval_jaxpr/ppermute | solution.py:268
  2525.8 143.7 %collective-permute-start.3 = (bf16[768,1536]{1,0:T(8,128)(2,1)}, bf16[768,1536]{1,0:T(8,128)(2,1)}, u32[]{:S(2)}, u32[]{:S(2)}) collective-permute-start(bf16[768,1536]{1,0:T(8,128)(2,1)} %broadcast_select_fusion.14), channel_id=1, source_target_pairs={{0,1},{1,2},{2,3},{4,5},{5,6},{6,7}} | collective-permute-start | bytes 7077896 | tf_op jit(solution)/shard_map/while/body/eval_jaxpr/ppermute | solution.py:267
  2532.5 143.5 %collective-permute-start.5 = (bf16[768,1536]{1,0:T(8,128)(2,1)}, bf16[768,1536]{1,0:T(8,128)(2,1)}, u32[]{:S(2)}, u32[]{:S(2)}) collective-permute-start(bf16[768,1536]{1,0:T(8,128)(2,1)} %broadcast_select_fusion.15), channel_id=1, source_target_pairs={{2,1},{6,5}} | collective-permute-start | bytes 7077896 | tf_op jit(solution)/shard_map/while/body/eval_jaxpr/ppermute | solution.py:268
  2690.4 143.7 %collective-permute-start.3 = (bf16[768,1536]{1,0:T(8,128)(2,1)}, bf16[768,1536]{1,0:T(8,128)(2,1)}, u32[]{:S(2)}, u32[]{:S(2)}) collective-permute-start(bf16[768,1536]{1,0:T(8,128)(2,1)} %broadcast_select_fusion.14), channel_id=1, source_target_pairs={{0,1},{1,2},{2,3},{4,5},{5,6},{6,7}} | collective-permute-start | bytes 7077896 | tf_op jit(solution)/shard_map/while/body/eval_jaxpr/ppermute | solution.py:267
  2697.2 143.4 %collective-permute-start.5 = (bf16[768,1536]{1,0:T(8,128)(2,1)}, bf16[768,1536]{1,0:T(8,128)(2,1)}, u32[]{:S(2)}, u32[]{:S(2)}) collective-permute-start(bf16[768,1536]{1,0:T(8,128)(2,1)} %broadcast_select_fusion.15), channel_id=1, source_target_pairs={{2,1},{6,5}} | collective-permute-start | bytes 7077896 | tf_op jit(solution)/shard_map/while/body/eval_jaxpr/ppermute | solution.py:268
  2855.0 143.7 %collective-permute-start.3 = (bf16[768,1536]{1,0:T(8,128)(2,1)}, bf16[768,1536]{1,0:T(8,128)(2,1)}, u32[]{:S(2)}, u32[]{:S(2)}) collective-permute-start(bf16[768,1536]{1,0:T(8,128)(2,1)} %broadcast_select_fusion.14), channel_id=1, source_target_pairs={{0,1},{1,2},{2,3},{4,5},{5,6},{6,7}} | collective-permute-start | bytes 7077896 | tf_op jit(solution)/shard_map/while/body/eval_jaxpr/ppermute | solution.py:267
  2861.8 143.4 %collective-permute-start.5 = (bf16[768,1536]{1,0:T(8,128)(2,1)}, bf16[768,1536]{1,0:T(8,128)(2,1)}, u32[]{:S(2)}, u32[]{:S(2)}) collective-permute-start(bf16[768,1536]{1,0:T(8,128)(2,1)} %broadcast_select_fusion.15), channel_id=1, source_target_pairs={{2,1},{6,5}} | collective-permute-start | bytes 7077896 | tf_op jit(solution)/shard_map/while/body/eval_jaxpr/ppermute | solution.py:268
  3019.5 143.6 %collective-permute-start.3 = (bf16[768,1536]{1,0:T(8,128)(2,1)}, bf16[768,1536]{1,0:T(8,128)(2,1)}, u32[]{:S(2)}, u32[]{:S(2)}) collective-permute-start(bf16[768,1536]{1,0:T(8,128)(2,1)} %broadcast_select_fusion.14), channel_id=1, source_target_pairs={{0,1},{1,2},{2,3},{4,5},{5,6},{6,7}} | collective-permute-start | bytes 7077896 | tf_op jit(solution)/shard_map/while/body/eval_jaxpr/ppermute | solution.py:267
  3026.3 143.3 %collective-permute-start.5 = (bf16[768,1536]{1,0:T(8,128)(2,1)}, bf16[768,1536]{1,0:T(8,128)(2,1)}, u32[]{:S(2)}, u32[]{:S(2)}) collective-permute-start(bf16[768,1536]{1,0:T(8,128)(2,1)} %broadcast_select_fusion.15), channel_id=1, source_target_pairs={{2,1},{6,5}} | collective-permute-start | bytes 7077896 | tf_op jit(solution)/shard_map/while/body/eval_jaxpr/ppermute | solution.py:268
  3168.3 8.6 collective-permute-start.4
  3184.2 143.7 %collective-permute-start.3 = (bf16[768,1536]{1,0:T(8,128)(2,1)}, bf16[768,1536]{1,0:T(8,128)(2,1)}, u32[]{:S(2)}, u32[]{:S(2)}) collective-permute-start(bf16[768,1536]{1,0:T(8,128)(2,1)} %broadcast_select_fusion.14), channel_id=1, source_target_pairs={{0,1},{1,2},{2,3},{4,5},{5,6},{6,7}} | collective-permute-start | bytes 7077896 | tf_op jit(solution)/shard_map/while/body/eval_jaxpr/ppermute | solution.py:267
  3191.0 143.4 %collective-permute-start.5 = (bf16[768,1536]{1,0:T(8,128)(2,1)}, bf16[768,1536]{1,0:T(8,128)(2,1)}, u32[]{:S(2)}, u32[]{:S(2)}) collective-permute-start(bf16[768,1536]{1,0:T(8,128)(2,1)} %broadcast_select_fusion.15), channel_id=1, source_target_pairs={{2,1},{6,5}} | collective-permute-start | bytes 7077896 | tf_op jit(solution)/shard_map/while/body/eval_jaxpr/ppermute | solution.py:268
  3333.1 8.6 collective-permute-start.4
  3348.9 143.6 %collective-permute-start.3 = (bf16[768,1536]{1,0:T(8,128)(2,1)}, bf16[768,1536]{1,0:T(8,128)(2,1)}, u32[]{:S(2)}, u32[]{:S(2)}) collective-permute-start(bf16[768,1536]{1,0:T(8,128)(2,1)} %broadcast_select_fusion.14), channel_id=1, source_target_pairs={{0,1},{1,2},{2,3},{4,5},{5,6},{6,7}} | collective-permute-start | bytes 7077896 | tf_op jit(solution)/shard_map/while/body/eval_jaxpr/ppermute | solution.py:267
  3355.7 143.3 %collective-permute-start.5 = (bf16[768,1536]{1,0:T(8,128)(2,1)}, bf16[768,1536]{1,0:T(8,128)(2,1)}, u32[]{:S(2)}, u32[]{:S(2)}) collective-permute-start(bf16[768,1536]{1,0:T(8,128)(2,1)} %broadcast_select_fusion.15), channel_id=1, source_target_pairs={{2,1},{6,5}} | collective-permute-start | bytes 7077896 | tf_op jit(solution)/shard_map/while/body/eval_jaxpr/ppermute | solution.py:268
  3497.8 8.7 collective-permute-start.4
  3513.7 143.8 %collective-permute-start.3 = (bf16[768,1536]{1,0:T(8,128)(2,1)}, bf16[768,1536]{1,0:T(8,128)(2,1)}, u32[]{:S(2)}, u32[]{:S(2)}) collective-permute-start(bf16[768,1536]{1,0:T(8,128)(2,1)} %broadcast_select_fusion.14), channel_id=1, source_target_pairs={{0,1},{1,2},{2,3},{4,5},{5,6},{6,7}} | collective-permute-start | bytes 7077896 | tf_op jit(solution)/shard_map/while/body/eval_jaxpr/ppermute | solution.py:267
  3520.5 143.5 %collective-permute-start.5 = (bf16[768,1536]{1,0:T(8,128)(2,1)}, bf16[768,1536]{1,0:T(8,128)(2,1)}, u32[]{:S(2)}, u32[]{:S(2)}) collective-permute-start(bf16[768,1536]{1,0:T(8,128)(2,1)} %broadcast_select_fusion.15), channel_id=1, source_target_pairs={{2,1},{6,5}} | collective-permute-start | bytes 7077896 | tf_op jit(solution)/shard_map/while/body/eval_jaxpr/ppermute | solution.py:268
  3678.2 143.7 %collective-permute-start.3 = (bf16[768,1536]{1,0:T(8,128)(2,1)}, bf16[768,1536]{1,0:T(8,128)(2,1)}, u32[]{:S(2)}, u32[]{:S(2)}) collective-permute-start(bf16[768,1536]{1,0:T(8,128)(2,1)} %broadcast_select_fusion.14), channel_id=1, source_target_pairs={{0,1},{1,2},{2,3},{4,5},{5,6},{6,7}} | collective-permute-start | bytes 7077896 | tf_op jit(solution)/shard_map/while/body/eval_jaxpr/ppermute | solution.py:267
  3685.0 143.4 %collective-permute-start.5 = (bf16[768,1536]{1,0:T(8,128)(2,1)}, bf16[768,1536]{1,0:T(8,128)(2,1)}, u32[]{:S(2)}, u32[]{:S(2)}) collective-permute-start(bf16[768,1536]{1,0:T(8,128)(2,1)} %broadcast_select_fusion.15), channel_id=1, source_target_pairs={{2,1},{6,5}} | collective-permute-start | bytes 7077896 | tf_op jit(solution)/shard_map/while/body/eval_jaxpr/ppermute | solution.py:268
  3827.1 8.5 collective-permute-start.4
  (117 other events, 1280.7 us)

commit v2 on v1

--- a/solution.py
+++ b/solution.py
@@ -10,6 +10,9 @@
 
 NORM_EPS = 1e-6
 ROWS = 128
+VMEM_BYTES = 48 * 1024 * 1024
+UP_ROWS = 256
+UP_COLS = 768
 
 
 def rms_norm(vals):
@@ -44,12 +47,44 @@
     )()
 
 
-def row_probs(query, keys, row0, scale):
-    scores = dot_nt(query, keys) * scale
-    row_id = row0 + lax.broadcasted_iota(jnp.int32, scores.shape, 0)
-    col_id = lax.broadcasted_iota(jnp.int32, scores.shape, 1)
-    scores = jnp.where(row_id >= col_id, scores, -1e30)
-    weights = jnp.exp(scores - jnp.max(scores, axis=-1, keepdims=True))
+def head_spans(lanes, head_dim):
+    spans = []
+    for lane0 in range(0, lanes, head_dim):
+        low = lane0 // 128 * 128
+        high = -(-(lane0 + head_dim) // 128) * 128
+        spans.append((low, high, lane0 - low, lane0 - low + head_dim))
+    return spans
+
+
+def keep_head(vals, first, last):
+    lane = lax.broadcasted_iota(jnp.int32, vals.shape, 1)
+    return jnp.where((lane >= first) & (lane < last), vals, jnp.zeros_like(vals))
+
+
+def merge_heads(pieces, spans, lanes):
+    blocks = []
+    for low in range(0, lanes, 128):
+        block = None
+        for piece, (span_low, span_high, first, _) in zip(pieces, spans):
+            if span_low <= low < span_high:
+                part = piece[:, low - span_low:low - span_low + 128]
+                if block is None:
+                    block = part
+                else:
+                    lane = lax.broadcasted_iota(jnp.int32, part.shape, 1)
+                    block = jnp.where(lane >= first + span_low - low, part, block)
+        blocks.append(block)
+    return jnp.concatenate(blocks, axis=1)
+
+
+def row_probs(query, keys, scale):
+    scores = dot_nt(query, keys)
+    n_rows, n_cols = scores.shape
+    row_id = lax.broadcasted_iota(jnp.int32, (n_rows, n_rows), 0)
+    col_id = lax.broadcasted_iota(jnp.int32, (n_rows, n_rows), 1)
+    diag = jnp.where(row_id >= col_id, scores[:, n_cols - n_rows:], -1e30)
+    scores = diag if n_cols == n_rows else jnp.concatenate([scores[:, :n_cols - n_rows], diag], axis=1)
+    weights = jnp.exp((scores - jnp.max(scores, axis=-1, keepdims=True)) * scale)
     return weights * (1.0 / jnp.sum(weights, axis=-1, keepdims=True))
 
 
@@ -57,57 +92,60 @@
     del slot_ref, old_ref
     seq_len, lanes = q_ref.shape[1:]
     scale = head_dim ** -0.5
+    spans = head_spans(lanes, head_dim)
     for row0 in range(0, seq_len, ROWS):
         n_cols = row0 + ROWS
         pieces = []
-        for lane0 in range(0, lanes, head_dim):
-            head = slice(lane0, lane0 + head_dim)
-            probs = row_probs(q_ref[0, row0:n_cols, head], k_ref[0, :n_cols, head], row0, scale)
-            pieces.append(dot_nn(probs.astype(jnp.bfloat16), v_ref[0, :n_cols, head]).astype(jnp.bfloat16))
-        out_ref[0, row0:n_cols, :] = jnp.concatenate(pieces, axis=1)
+        for low, high, first, last in spans:
+            query = keep_head(q_ref[0, row0:n_cols, low:high], first, last)
+            probs = row_probs(query, k_ref[0, :n_cols, low:high], scale)
+            pieces.append(dot_nn(probs.astype(jnp.bfloat16), v_ref[0, :n_cols, low:high]))
+        out_ref[0, row0:n_cols, :] = merge_heads(pieces, spans, lanes).astype(jnp.bfloat16)
 
 
 def attn_bwd_kernel(head_dim, n_groups, slot_ref, q_ref, k_ref, v_ref, dctx_ref, old_ref, out_ref):
     del slot_ref, old_ref
     seq_len, lanes = q_ref.shape[1:]
     scale = head_dim ** -0.5
+    spans = head_spans(lanes, head_dim)
     n_rows = seq_len // ROWS
-    dq_rows = [[] for _ in range(n_rows)]
-    dk_rows = [[] for _ in range(n_rows)]
-    dv_rows = [[] for _ in range(n_rows)]
-    for lane0 in range(0, lanes, head_dim):
-        head = slice(lane0, lane0 + head_dim)
-        dk_sum = [None] * n_rows
-        dv_sum = [None] * n_rows
+    dq_all = []
+    dk_all = []
+    dv_all = []
+    for low, high, first, last in spans:
+        dq_rows = []
+        probs_rows = []
+        scores_rows = []
         for row_blk in range(n_rows):
             row0 = row_blk * ROWS
             n_cols = row0 + ROWS
-            query = q_ref[0, row0:n_cols, head]
-            keys = k_ref[0, :n_cols, head]
-            dctx = dctx_ref[row0:n_cols, head]
-            probs = row_probs(query, keys, row0, scale)
-            d_probs = dot_nt(dctx, v_ref[0, :n_cols, head])
+            query = keep_head(q_ref[0, row0:n_cols, low:high], first, last)
+            dctx = keep_head(dctx_ref[row0:n_cols, low:high], first, last)
+            keys = k_ref[0, :n_cols, low:high]
+            probs = row_probs(query, keys, scale)
+            d_probs = dot_nt(dctx, v_ref[0, :n_cols, low:high])
             delta = jnp.sum(d_probs * probs, axis=-1, keepdims=True)
             d_scores = (probs * (d_probs - delta) * scale).astype(jnp.bfloat16)
-            dq_rows[row_blk].append(dot_nn(d_scores, keys).astype(jnp.bfloat16))
-            dk_part = dot_tn(d_scores, query)
-            dv_part = dot_tn(probs.astype(jnp.bfloat16), dctx)
-            for col_blk in range(row_blk + 1):
-                cols = slice(col_blk * ROWS, (col_blk + 1) * ROWS)
-                if dk_sum[col_blk] is None:
-                    dk_sum[col_blk] = dk_part[cols]
-                    dv_sum[col_blk] = dv_part[cols]
-                else:
-                    dk_sum[col_blk] = dk_sum[col_blk] + dk_part[cols]
-                    dv_sum[col_blk] = dv_sum[col_blk] + dv_part[cols]
-        for row_blk in range(n_rows):
-            dk_rows[row_blk].append(dk_sum[row_blk].astype(jnp.bfloat16))
-            dv_rows[row_blk].append(dv_sum[row_blk].astype(jnp.bfloat16))
+            dq_rows.append(dot_nn(d_scores, keys))
+            probs_rows.append(probs.astype(jnp.bfloat16))
+            scores_rows.append(d_scores)
+        dk_cols = []
+        dv_cols = []
+        for col_blk in range(n_rows):
+            cols = slice(col_blk * ROWS, (col_blk + 1) * ROWS)
+            below = jnp.concatenate([scores_rows[r][:, cols] for r in range(col_blk, n_rows)], axis=0)
+            dk_cols.append(dot_tn(below, q_ref[0, col_blk * ROWS:, low:high]))
+            below = jnp.concatenate([probs_rows[r][:, cols] for r in range(col_blk, n_rows)], axis=0)
+            dv_cols.append(dot_tn(below, dctx_ref[col_blk * ROWS:, low:high]))
+        dq_all.append(dq_rows)
+        dk_all.append(dk_cols)
+        dv_all.append(dv_cols)
     group = pl.program_id(1)
-    for kind, rows in enumerate((dq_rows, dk_rows, dv_rows)):
+    for kind, heads in enumerate((dq_all, dk_all, dv_all)):
         lane = pl.multiple_of((kind * n_groups + group) * lanes, 128)
         for row_blk in range(n_rows):
-            out_ref[0, row_blk * ROWS:(row_blk + 1) * ROWS, pl.ds(lane, lanes)] = jnp.concatenate(rows[row_blk], axis=1)
+            merged = merge_heads([rows[row_blk] for rows in heads], spans, lanes).astype(jnp.bfloat16)
+            out_ref[0, row_blk * ROWS:(row_blk + 1) * ROWS, pl.ds(lane, lanes)] = merged
 
 
 def attention_calls(n_slots, micro_b, seq_len, width, n_heads):
@@ -133,7 +171,7 @@
             ),
             input_output_aliases={4: 0},
             cost_estimate=pl.CostEstimate(flops=flops * 6, bytes_accessed=rows * width * 8, transcendentals=0),
-            compiler_params=pltpu.CompilerParams(vmem_limit_bytes=32 * 1024 * 1024),
+            compiler_params=pltpu.CompilerParams(vmem_limit_bytes=VMEM_BYTES),
             name='attn_fwd',
         )(slot.reshape(1), qkv_st, qkv_st, qkv_st, ctx_st)
 
@@ -149,11 +187,72 @@
             ),
             input_output_aliases={5: 0},
             cost_estimate=pl.CostEstimate(flops=flops * 12, bytes_accessed=rows * width * 14, transcendentals=0),
-            compiler_params=pltpu.CompilerParams(vmem_limit_bytes=40 * 1024 * 1024),
+            compiler_params=pltpu.CompilerParams(vmem_limit_bytes=VMEM_BYTES),
             name='attn_bwd',
         )(slot.reshape(1), qkv_st, qkv_st, qkv_st, dctx, dqkv_st)
 
     return fwd, bwd
+
+
+def up_kernel(slot_ref, n2_ref, w_ref, old_pre_ref, old_u_ref, pre_ref, u_ref):
+    del slot_ref, old_pre_ref, old_u_ref
+    for row0 in range(0, n2_ref.shape[1], UP_ROWS):
+        rows = slice(row0, row0 + UP_ROWS)
+        pre_act = dot_nn(n2_ref[0, rows, :], w_ref[...])
+        pre_ref[0, rows, :] = pre_act
+        u_ref[0, rows, :] = gelu_tanh(pre_act).astype(jnp.bfloat16)
+
+
+def d_pre_kernel(slot_ref, g_ref, w_ref, pre_ref, old_ref, out_ref):
+    del slot_ref, old_ref
+    for row0 in range(0, g_ref.shape[1], UP_ROWS):
+        rows = slice(row0, row0 + UP_ROWS)
+        d_upper = dot_nt(g_ref[0, rows, :], w_ref[...])
+        out_ref[0, rows, :] = jax.vjp(gelu_tanh, pre_ref[0, rows, :])[1](d_upper)[0].astype(jnp.bfloat16)
+
+
+def hidden_calls(n_slots, rows, width, hidden):
+    whole = pl.BlockSpec((1, rows, width), lambda j, slot: (slot[0], 0, 0))
+    piece = pl.BlockSpec((1, rows, UP_COLS), lambda j, slot: (slot[0], 0, j))
+    anywhere = pl.BlockSpec(memory_space=pl.ANY)
+    params = pltpu.CompilerParams(vmem_limit_bytes=VMEM_BYTES)
+    cost = pl.CostEstimate(flops=2 * rows * width * hidden, bytes_accessed=hidden * (2 * width + 6 * rows), transcendentals=0)
+    stack16 = jax.ShapeDtypeStruct((n_slots, rows, hidden), jnp.bfloat16)
+    stack32 = jax.ShapeDtypeStruct((n_slots, rows, hidden), jnp.float32)
+
+    def up(slot, n2_st, w_up, pre_st, u_st):
+        return pl.pallas_call(
+            up_kernel,
+            out_shape=(stack32, stack16),
+            grid_spec=pltpu.PrefetchScalarGridSpec(
+                num_scalar_prefetch=1,
+                grid=(hidden // UP_COLS,),
+                in_specs=[whole, pl.BlockSpec((width, UP_COLS), lambda j, slot: (0, j)), anywhere, anywhere],
+                out_specs=(piece, piece),
+            ),
+            input_output_aliases={3: 0, 4: 1},
+            cost_estimate=cost,
+            compiler_params=params,
+            name='up',
+        )(slot.reshape(1), n2_st, w_up, pre_st, u_st)
+
+    def d_pre(slot, g_st, w_down, pre_st, dpre_st):
+        return pl.pallas_call(
+            d_pre_kernel,
+            out_shape=stack16,
+            grid_spec=pltpu.PrefetchScalarGridSpec(
+                num_scalar_prefetch=1,
+                grid=(hidden // UP_COLS,),
+                in_specs=[whole, pl.BlockSpec((UP_COLS, width), lambda j, slot: (j, 0)), piece, anywhere],
+                out_specs=piece,
+            ),
+            input_output_aliases={4: 0},
+            cost_estimate=cost,
+            compiler_params=params,
+            name='d_pre',
+        )(slot.reshape(1), g_st, w_down, pre_st, dpre_st)
+
+    return up, d_pre
 
 
 def put(stack, value, slot):
@@ -190,6 +289,7 @@
         w_up = w_up[0]
         w_down = w_down[0]
         attn_fwd, attn_bwd = attention_calls(n_micro, micro_b, seq_len, width, n_heads)
+        up, d_pre = hidden_calls(n_micro, rows, width, hidden)
         stage_idx = lax.axis_index('stage')
         data_idx = lax.axis_index('data')
         is_first = stage_idx == 0
@@ -244,9 +344,7 @@
             hidden32 = hidden16.astype(jnp.float32)
             normed2 = rms_norm(hidden32).astype(bf16)
             n2_st = put(n2_st, normed2, slot)
-            pre_act = dot_nn(normed2, w_up)
-            pre_st = put(pre_st, pre_act, slot)
-            u_st = lax.optimization_barrier(put(u_st, gelu_tanh(pre_act).astype(bf16), slot))
+            pre_st, u_st = up(slot, n2_st, w_up, pre_st, u_st)
             act_out = (hidden32 + dot_nn(get(u_st, slot), w_down)).astype(bf16)
             error = act_out.astype(jnp.float32) - outside.astype(jnp.float32)
             losses = put(losses, 0.5 * jnp.sum(error * error) * loss_norm, slot)
@@ -270,10 +368,8 @@
             slot = slot_of(jnp.clip(from_last, 0, n_micro - 1))
             grad_out = jnp.where(is_last, get(g_st, slot), cur_in)
             g_st = put(g_st, grad_out, slot)
-            d_upper = dot_nt(grad_out, w_down)
-            d_pre = jax.vjp(gelu_tanh, get(pre_st, slot))[1](d_upper)[0].astype(bf16)
-            dpre_st = put(dpre_st, d_pre, slot)
-            d_normed2 = dot_nt(d_pre, w_up)
+            dpre_st = d_pre(slot, g_st, w_down, pre_st, dpre_st)
+            d_normed2 = dot_nt(get(dpre_st, slot), w_up)
             hidden32 = get(h_st, slot).astype(jnp.float32)
             d_hidden = grad_out.astype(jnp.float32) + jax.vjp(rms_norm, hidden32)[1](d_normed2)[0]
             d_hidden16 = d_hidden.astype(bf16)
@@ -303,7 +399,7 @@
         d_up = weight_grad(n2_st, dpre_st)[None]
         d_down = weight_grad(u_st, g_st)[None]
         loss = lax.psum(jnp.where(is_last, jnp.sum(losses), 0.0), 'stage').reshape(1)
-        d_embeds = dx_st[:n_own].reshape(n_own, micro_b, seq_len, width)
+        d_embeds = dx_st[:n_own].reshape(embeds.shape)
         return loss, d_qkv, d_out, d_up, d_down, d_embeds
 
     return jax.shard_map(per_device, mesh=mesh, in_specs=(act_spec, act_spec, weight_spec, weight_spec, weight_spec, weight_spec), out_specs=(P('rep'), weight_spec, weight_spec, weight_spec, weight_spec, act_spec), check_vma=False)

time: 4270 us -> 4190 us (0.981)
  matrix products: 2160 us -> 1490 us
  Pallas kernels: 992 us -> 1520 us
  starting transfers between devices: 187 us -> 332 us
  local copies, waits for them, and re-layouts: 358 us -> 224 us
  other arithmetic: 442 us -> 488 us
    pallas_call x0 -> x24, Pallas kernels: none -> 620 us  [the longest x12 325 us: d_pre(): pl.pallas_call(d_pre_kernel, out_shape=stack16, grid_spec=pltpu.PrefetchS...]
    dot_general x48 -> x36, matrix products: 913 us -> 546 us  [dot_nt(): lax.dot_general(lhs, rhs, (((1,), (1,)), ((), ())), preferred_element_typ...]
    dot_general x48 -> x36, matrix products: 850 us -> 539 us  [dot_nn(): lax.dot_general(lhs, rhs, (((1,), (0,)), ((), ())), preferred_element_typ...]
    ppermute x12, starting transfers between devices: 47.7 us -> 182 us  [fwd_tick(): fast_in = lax.ppermute(act_out, 'stage', fast_fwd)]
    dynamic_update_slice x36, local copies, waits for them, and re-layouts: 193 us -> 59.1 us  [put(): return lax.dynamic_update_index_in_dim(stack, value, slot, 0)]
    pallas_call x12, Pallas kernels: 595 us -> 534 us  [bwd(): pl.pallas_call(functools.partial(attn_bwd_kernel, head_dim, n_groups), ou...]
    dynamic_update_slice x48 -> x60, other arithmetic: 197 us -> 241 us  [put(): return lax.dynamic_update_index_in_dim(stack, value, slot, 0)]
    while x36 -> x48, other arithmetic: 93.5 us -> 95.1 us
  transfers between devices with their start and end apart: 72 -> 72, of which waited for: 12 -> 12; matrix products, arithmetic and copies ran while one was open for 55% -> 37% of each run, Pallas kernels for 23% -> 36%
where the time goes in v2:
time: 4190 us; the launch traced here: 4170 us
  Pallas kernels  1520 us (36%)
  matrix products  1490 us (36%)
  other arithmetic  488 us (12%)
  starting transfers between devices  332 us (8%)
  local copies, waits for them, and re-layouts  224 us (5%)
  waiting for transfers between devices  85.7 us (2%)
    dot_general x36, matrix products, dot_nt(): lax.dot_general(lhs, rhs, (((1,), (1,)), ((), ())), preferred_element_typ...  546 us
    dot_general x36, matrix products, dot_nn(): lax.dot_general(lhs, rhs, (((1,), (0,)), ((), ())), preferred_element_typ...  539 us
    pallas_call x12, Pallas kernels, bwd(): pl.pallas_call(functools.partial(attn_bwd_kernel, head_dim, n_groups), ou...  534 us
    dot_general x4, matrix products, dot_tn(): lax.dot_general(lhs, rhs, (((0,), (0,)), ((), ())), preferred_element_typ...  401 us
    pallas_call x12, Pallas kernels, fwd(): pl.pallas_call(functools.partial(attn_fwd_kernel, head_dim), out_shape=ja...  366 us
    pallas_call x12, Pallas kernels, d_pre(): pl.pallas_call(d_pre_kernel, out_shape=stack16, grid_spec=pltpu.PrefetchS...  325 us
    pallas_call x12, Pallas kernels, up(): pl.pallas_call(up_kernel, out_shape=(stack32, stack16), grid_spec=pltpu.P...  294 us
    dynamic_update_slice x60, other arithmetic, put(): return lax.dynamic_update_index_in_dim(stack, value, slot, 0)  241 us
  transfers between devices with their start and end apart: 72, of which 12 were waited for; matrix products, arithmetic and copies ran while one was open for 37% of the time, Pallas kernels for 36%

profile of v2, /device:TPU:0, one launch (start us, length us, event | category | flops | bytes accessed | tf_op | source)
XLA Modules:
  0.0 4171.4 jit_solution(9658556247129241498)
XLA Ops:
  18.3 1813.0 %while.70 = (s32[]{:T(128)}, bf16[768,1536]{1,0:T(8,128)(2,1)}, bf16[768,1536]{1,0:T(8,128)(2,1)}, bf16[8,768,1536]{2,1,0:T(8,128)(2,1)}, bf16[8,768,1536]{2,1,0...) while((s32[]{:T(128)}, bf16[768,1536]{1,0:T(8,128)(2,1)}, ...), condition=%wide.region_4.5_spmd.clone, body=%wide.region_0.4_spmd.clone.sunk | while | flops 54405365760 | bytes 290248448 | solution.py:360
  47.1 30.5 attn_fwd.8
  86.3 24.5 up.8
  110.8 22.4 fusion.79
  185.7 30.5 attn_fwd.8
  224.9 24.6 up.8
  249.4 22.4 fusion.79
  337.6 30.5 attn_fwd.8
  376.8 24.5 up.8
  401.3 22.4 fusion.79
  489.8 30.5 attn_fwd.8
  529.0 24.5 up.8
  641.7 30.5 attn_fwd.8
  680.9 24.5 up.8
  793.9 30.5 attn_fwd.8
  833.1 24.5 up.8
  857.6 22.5 fusion.79
  945.7 30.5 attn_fwd.8
  985.0 24.6 up.8
  1098.0 30.5 attn_fwd.8
  1137.2 24.6 up.8
  1161.8 22.4 fusion.79
  1250.4 30.5 attn_fwd.8
  1289.6 24.6 up.8
  1314.2 22.4 fusion.79
  1402.3 30.5 attn_fwd.8
  1441.5 24.6 up.8
  1466.1 22.4 fusion.79
  1554.5 30.5 attn_fwd.8
  1593.7 24.6 up.8
  1618.2 22.4 fusion.79
  1706.6 30.5 attn_fwd.8
  1745.8 24.6 up.8
  1770.4 22.4 fusion.79
  1831.3 1917.8 %while.71 = (s32[]{:T(128)}, bf16[768,1536]{1,0:T(8,128)(2,1)}, bf16[768,1536]{1,0:T(8,128)(2,1)}, bf16[768,1536]{1,0:T(8,128)(2,1)}, bf16[8,768,1536]{2,1,0:T(8...) while((s32[]{:T(128)}, bf16[768,1536]{1,0:T(8,128)(2,1)}, ...), condition=%wide.region_12.13_spmd.clone, body=%wide.region_7.12_spmd.clone.sunk | while | flops 65271107584 | bytes 292605184 | solution.py:391
  1868.7 27.1 d_pre.8
  1931.6 44.5 %attn_bwd.8 = bf16[8,768,4608]{2,1,0:T(8,128)(2,1)} custom-call(s32[1]{0:T(128)} %bitcast.153.slot_ref, bf16[8,768,4608]{2,1,0:T(8,128)(2,1)} %get-tuple-element.1848.q_ref.k_ref.v_ref, bf16[8,768,4608]{2,1,0:T(8,128)(2,1)} %get-tuple-element.1848.q_ref.k_ref.v_ref, ...), custom_call_target="tpu_custom_call", output_to_operand_aliasing={{}: (5, {})} | custom-call | flops 21743271936 | bytes 16515072 | tf_op jit(solution)/shard_map/while/body/eval_jaxpr/attn_bwd/pallas_call | solution.py:179
  2025.0 27.1 d_pre.8
  2087.9 44.5 %attn_bwd.8 = bf16[8,768,4608]{2,1,0:T(8,128)(2,1)} custom-call(s32[1]{0:T(128)} %bitcast.153.slot_ref, bf16[8,768,4608]{2,1,0:T(8,128)(2,1)} %get-tuple-element.1848.q_ref.k_ref.v_ref, bf16[8,768,4608]{2,1,0:T(8,128)(2,1)} %get-tuple-element.1848.q_ref.k_ref.v_ref, ...), custom_call_target="tpu_custom_call", output_to_operand_aliasing={{}: (5, {})} | custom-call | flops 21743271936 | bytes 16515072 | tf_op jit(solution)/shard_map/while/body/eval_jaxpr/attn_bwd/pallas_call | solution.py:179
  2182.8 27.1 d_pre.8
  2245.6 44.5 %attn_bwd.8 = bf16[8,768,4608]{2,1,0:T(8,128)(2,1)} custom-call(s32[1]{0:T(128)} %bitcast.153.slot_ref, bf16[8,768,4608]{2,1,0:T(8,128)(2,1)} %get-tuple-element.1848.q_ref.k_ref.v_ref, bf16[8,768,4608]{2,1,0:T(8,128)(2,1)} %get-tuple-element.1848.q_ref.k_ref.v_ref, ...), custom_call_target="tpu_custom_call", output_to_operand_aliasing={{}: (5, {})} | custom-call | flops 21743271936 | bytes 16515072 | tf_op jit(solution)/shard_map/while/body/eval_jaxpr/attn_bwd/pallas_call | solution.py:179
  2340.9 27.1 d_pre.8
  2403.8 44.5 %attn_bwd.8 = bf16[8,768,4608]{2,1,0:T(8,128)(2,1)} custom-call(s32[1]{0:T(128)} %bitcast.153.slot_ref, bf16[8,768,4608]{2,1,0:T(8,128)(2,1)} %get-tuple-element.1848.q_ref.k_ref.v_ref, bf16[8,768,4608]{2,1,0:T(8,128)(2,1)} %get-tuple-element.1848.q_ref.k_ref.v_ref, ...), custom_call_target="tpu_custom_call", output_to_operand_aliasing={{}: (5, {})} | custom-call | flops 21743271936 | bytes 16515072 | tf_op jit(solution)/shard_map/while/body/eval_jaxpr/attn_bwd/pallas_call | solution.py:179
  2499.2 27.1 d_pre.8
  2562.0 44.5 %attn_bwd.8 = bf16[8,768,4608]{2,1,0:T(8,128)(2,1)} custom-call(s32[1]{0:T(128)} %bitcast.153.slot_ref, bf16[8,768,4608]{2,1,0:T(8,128)(2,1)} %get-tuple-element.1848.q_ref.k_ref.v_ref, bf16[8,768,4608]{2,1,0:T(8,128)(2,1)} %get-tuple-element.1848.q_ref.k_ref.v_ref, ...), custom_call_target="tpu_custom_call", output_to_operand_aliasing={{}: (5, {})} | custom-call | flops 21743271936 | bytes 16515072 | tf_op jit(solution)/shard_map/while/body/eval_jaxpr/attn_bwd/pallas_call | solution.py:179
  2657.6 27.1 d_pre.8
  2720.4 44.6 %attn_bwd.8 = bf16[8,768,4608]{2,1,0:T(8,128)(2,1)} custom-call(s32[1]{0:T(128)} %bitcast.153.slot_ref, bf16[8,768,4608]{2,1,0:T(8,128)(2,1)} %get-tuple-element.1848.q_ref.k_ref.v_ref, bf16[8,768,4608]{2,1,0:T(8,128)(2,1)} %get-tuple-element.1848.q_ref.k_ref.v_ref, ...), custom_call_target="tpu_custom_call", output_to_operand_aliasing={{}: (5, {})} | custom-call | flops 21743271936 | bytes 16515072 | tf_op jit(solution)/shard_map/while/body/eval_jaxpr/attn_bwd/pallas_call | solution.py:179
  2815.8 27.1 d_pre.8
  2878.6 44.6 %attn_bwd.8 = bf16[8,768,4608]{2,1,0:T(8,128)(2,1)} custom-call(s32[1]{0:T(128)} %bitcast.153.slot_ref, bf16[8,768,4608]{2,1,0:T(8,128)(2,1)} %get-tuple-element.1848.q_ref.k_ref.v_ref, bf16[8,768,4608]{2,1,0:T(8,128)(2,1)} %get-tuple-element.1848.q_ref.k_ref.v_ref, ...), custom_call_target="tpu_custom_call", output_to_operand_aliasing={{}: (5, {})} | custom-call | flops 21743271936 | bytes 16515072 | tf_op jit(solution)/shard_map/while/body/eval_jaxpr/attn_bwd/pallas_call | solution.py:179
  2973.9 27.1 d_pre.8
  3001.0 22.4 fusion.84
  3036.8 44.5 %attn_bwd.8 = bf16[8,768,4608]{2,1,0:T(8,128)(2,1)} custom-call(s32[1]{0:T(128)} %bitcast.153.slot_ref, bf16[8,768,4608]{2,1,0:T(8,128)(2,1)} %get-tuple-element.1848.q_ref.k_ref.v_ref, bf16[8,768,4608]{2,1,0:T(8,128)(2,1)} %get-tuple-element.1848.q_ref.k_ref.v_ref, ...), custom_call_target="tpu_custom_call", output_to_operand_aliasing={{}: (5, {})} | custom-call | flops 21743271936 | bytes 16515072 | tf_op jit(solution)/shard_map/while/body/eval_jaxpr/attn_bwd/pallas_call | solution.py:179
  3132.4 27.1 d_pre.8
  3195.3 44.5 %attn_bwd.8 = bf16[8,768,4608]{2,1,0:T(8,128)(2,1)} custom-call(s32[1]{0:T(128)} %bitcast.153.slot_ref, bf16[8,768,4608]{2,1,0:T(8,128)(2,1)} %get-tuple-element.1848.q_ref.k_ref.v_ref, bf16[8,768,4608]{2,1,0:T(8,128)(2,1)} %get-tuple-element.1848.q_ref.k_ref.v_ref, ...), custom_call_target="tpu_custom_call", output_to_operand_aliasing={{}: (5, {})} | custom-call | flops 21743271936 | bytes 16515072 | tf_op jit(solution)/shard_map/while/body/eval_jaxpr/attn_bwd/pallas_call | solution.py:179
  3290.2 27.1 d_pre.8
  3353.0 44.5 %attn_bwd.8 = bf16[8,768,4608]{2,1,0:T(8,128)(2,1)} custom-call(s32[1]{0:T(128)} %bitcast.153.slot_ref, bf16[8,768,4608]{2,1,0:T(8,128)(2,1)} %get-tuple-element.1848.q_ref.k_ref.v_ref, bf16[8,768,4608]{2,1,0:T(8,128)(2,1)} %get-tuple-element.1848.q_ref.k_ref.v_ref, ...), custom_call_target="tpu_custom_call", output_to_operand_aliasing={{}: (5, {})} | custom-call | flops 21743271936 | bytes 16515072 | tf_op jit(solution)/shard_map/while/body/eval_jaxpr/attn_bwd/pallas_call | solution.py:179
  3448.6 27.1 d_pre.8
  3511.4 44.5 %attn_bwd.8 = bf16[8,768,4608]{2,1,0:T(8,128)(2,1)} custom-call(s32[1]{0:T(128)} %bitcast.153.slot_ref, bf16[8,768,4608]{2,1,0:T(8,128)(2,1)} %get-tuple-element.1848.q_ref.k_ref.v_ref, bf16[8,768,4608]{2,1,0:T(8,128)(2,1)} %get-tuple-element.1848.q_ref.k_ref.v_ref, ...), custom_call_target="tpu_custom_call", output_to_operand_aliasing={{}: (5, {})} | custom-call | flops 21743271936 | bytes 16515072 | tf_op jit(solution)/shard_map/while/body/eval_jaxpr/attn_bwd/pallas_call | solution.py:179
  3606.9 27.1 d_pre.8
  3669.7 44.6 %attn_bwd.8 = bf16[8,768,4608]{2,1,0:T(8,128)(2,1)} custom-call(s32[1]{0:T(128)} %bitcast.153.slot_ref, bf16[8,768,4608]{2,1,0:T(8,128)(2,1)} %get-tuple-element.1848.q_ref.k_ref.v_ref, bf16[8,768,4608]{2,1,0:T(8,128)(2,1)} %get-tuple-element.1848.q_ref.k_ref.v_ref, ...), custom_call_target="tpu_custom_call", output_to_operand_aliasing={{}: (5, {})} | custom-call | flops 21743271936 | bytes 16515072 | tf_op jit(solution)/shard_map/while/body/eval_jaxpr/attn_bwd/pallas_call | solution.py:179
  3749.1 130.6 %convolution_bitcast_fusion = f32[6144,1536]{1,0:T(8,128)} fusion(bf16[8,768,6144]{2,1,0:T(8,128)(2,1)} %get-tuple-element.1090, bf16[8,768,1536]{2,1,0:T(8,128)(2,1)} %get-tuple-element.1091), kind=kOutput, calls=%fused_computation.81 | convolution fusion | flops 115964116992 | bytes 132120576 | tf_op jit(solution)/shard_map/dot_general | solution.py:35
  3879.7 132.8 %convolution_bitcast_fusion.1 = f32[1536,6144]{1,0:T(8,128)} fusion(bf16[8,768,1536]{2,1,0:T(8,128)(2,1)} %get-tuple-element.1088, bf16[8,768,6144]{2,1,0:T(8,128)(2,1)} %get-tuple-element.1089), kind=kOutput, calls=%fused_computation.82 | convolution fusion | flops 115964116992 | bytes 132120576 | tf_op jit(solution)/shard_map/dot_general | solution.py:35
  4012.5 37.9 convolution_bitcast_fusion.3
  4050.4 100.1 %convolution_bitcast_fusion.2 = f32[4608,1536]{1,0:T(8,128)} fusion(bf16[8,768,4608]{2,1,0:T(8,128)(2,1)} %get-tuple-element.1084, bf16[8,768,1536]{2,1,0:T(8,128)(2,1)} %get-tuple-element.1085), kind=kOutput, calls=%fused_computation.83 | convolution fusion | flops 86973087744 | bytes 103809024 | tf_op jit(solution)/shard_map/dot_general | solution.py:35
  (880 shorter events, 2001.3 us)
Async XLA Ops:
  22.4 128.4 %collective-permute-start.2 = (bf16[768,1536]{1,0:T(8,128)(2,1)}, bf16[768,1536]{1,0:T(8,128)(2,1)}, u32[]{:S(2)}, u32[]{:S(2)}) collective-permute-start(bf16[768,1536]{1,0:T(8,128)(2,1)} %get-tuple-element.1636), channel_id=1, source_target_pairs={{0,4},{3,7},{4,0},{7,3}} | collective-permute-start | bytes 7077896 | tf_op jit(solution)/shard_map/while/body/eval_jaxpr/ppermute | solution.py:330
  133.1 20.8 collective-permute-start.1
  137.4 16.6 collective-permute-start
  162.1 140.7 %collective-permute-start.2 = (bf16[768,1536]{1,0:T(8,128)(2,1)}, bf16[768,1536]{1,0:T(8,128)(2,1)}, u32[]{:S(2)}, u32[]{:S(2)}) collective-permute-start(bf16[768,1536]{1,0:T(8,128)(2,1)} %get-tuple-element.1636), channel_id=1, source_target_pairs={{0,4},{3,7},{4,0},{7,3}} | collective-permute-start | bytes 7077896 | tf_op jit(solution)/shard_map/while/body/eval_jaxpr/ppermute | solution.py:330
  271.8 34.1 collective-permute-start.1
  289.4 16.6 collective-permute-start
  314.0 140.9 %collective-permute-start.2 = (bf16[768,1536]{1,0:T(8,128)(2,1)}, bf16[768,1536]{1,0:T(8,128)(2,1)}, u32[]{:S(2)}, u32[]{:S(2)}) collective-permute-start(bf16[768,1536]{1,0:T(8,128)(2,1)} %get-tuple-element.1636), channel_id=1, source_target_pairs={{0,4},{3,7},{4,0},{7,3}} | collective-permute-start | bytes 7077896 | tf_op jit(solution)/shard_map/while/body/eval_jaxpr/ppermute | solution.py:330
  423.7 34.5 collective-permute-start.1
  441.5 16.6 collective-permute-start
  466.5 140.5 %collective-permute-start.2 = (bf16[768,1536]{1,0:T(8,128)(2,1)}, bf16[768,1536]{1,0:T(8,128)(2,1)}, u32[]{:S(2)}, u32[]{:S(2)}) collective-permute-start(bf16[768,1536]{1,0:T(8,128)(2,1)} %get-tuple-element.1636), channel_id=1, source_target_pairs={{0,4},{3,7},{4,0},{7,3}} | collective-permute-start | bytes 7077896 | tf_op jit(solution)/shard_map/while/body/eval_jaxpr/ppermute | solution.py:330
  575.8 34.4 collective-permute-start.1
  593.6 16.6 collective-permute-start
  618.4 140.8 %collective-permute-start.2 = (bf16[768,1536]{1,0:T(8,128)(2,1)}, bf16[768,1536]{1,0:T(8,128)(2,1)}, u32[]{:S(2)}, u32[]{:S(2)}) collective-permute-start(bf16[768,1536]{1,0:T(8,128)(2,1)} %get-tuple-element.1636), channel_id=1, source_target_pairs={{0,4},{3,7},{4,0},{7,3}} | collective-permute-start | bytes 7077896 | tf_op jit(solution)/shard_map/while/body/eval_jaxpr/ppermute | solution.py:330
  727.7 34.7 collective-permute-start.1
  745.8 16.6 collective-permute-start
  770.5 140.6 %collective-permute-start.2 = (bf16[768,1536]{1,0:T(8,128)(2,1)}, bf16[768,1536]{1,0:T(8,128)(2,1)}, u32[]{:S(2)}, u32[]{:S(2)}) collective-permute-start(bf16[768,1536]{1,0:T(8,128)(2,1)} %get-tuple-element.1636), channel_id=1, source_target_pairs={{0,4},{3,7},{4,0},{7,3}} | collective-permute-start | bytes 7077896 | tf_op jit(solution)/shard_map/while/body/eval_jaxpr/ppermute | solution.py:330
  880.1 34.3 collective-permute-start.1
  897.7 16.7 collective-permute-start
  922.5 140.8 %collective-permute-start.2 = (bf16[768,1536]{1,0:T(8,128)(2,1)}, bf16[768,1536]{1,0:T(8,128)(2,1)}, u32[]{:S(2)}, u32[]{:S(2)}) collective-permute-start(bf16[768,1536]{1,0:T(8,128)(2,1)} %get-tuple-element.1636), channel_id=1, source_target_pairs={{0,4},{3,7},{4,0},{7,3}} | collective-permute-start | bytes 7077896 | tf_op jit(solution)/shard_map/while/body/eval_jaxpr/ppermute | solution.py:330
  1031.9 34.7 collective-permute-start.1
  1050.0 16.6 collective-permute-start
  1074.7 141.0 %collective-permute-start.2 = (bf16[768,1536]{1,0:T(8,128)(2,1)}, bf16[768,1536]{1,0:T(8,128)(2,1)}, u32[]{:S(2)}, u32[]{:S(2)}) collective-permute-start(bf16[768,1536]{1,0:T(8,128)(2,1)} %get-tuple-element.1636), channel_id=1, source_target_pairs={{0,4},{3,7},{4,0},{7,3}} | collective-permute-start | bytes 7077896 | tf_op jit(solution)/shard_map/while/body/eval_jaxpr/ppermute | solution.py:330
  1184.2 34.7 collective-permute-start.1
  1202.3 16.6 collective-permute-start
  1227.0 140.6 %collective-permute-start.2 = (bf16[768,1536]{1,0:T(8,128)(2,1)}, bf16[768,1536]{1,0:T(8,128)(2,1)}, u32[]{:S(2)}, u32[]{:S(2)}) collective-permute-start(bf16[768,1536]{1,0:T(8,128)(2,1)} %get-tuple-element.1636), channel_id=1, source_target_pairs={{0,4},{3,7},{4,0},{7,3}} | collective-permute-start | bytes 7077896 | tf_op jit(solution)/shard_map/while/body/eval_jaxpr/ppermute | solution.py:330
  1336.6 34.3 collective-permute-start.1
  1354.2 16.6 collective-permute-start
  1378.9 140.8 %collective-permute-start.2 = (bf16[768,1536]{1,0:T(8,128)(2,1)}, bf16[768,1536]{1,0:T(8,128)(2,1)}, u32[]{:S(2)}, u32[]{:S(2)}) collective-permute-start(bf16[768,1536]{1,0:T(8,128)(2,1)} %get-tuple-element.1636), channel_id=1, source_target_pairs={{0,4},{3,7},{4,0},{7,3}} | collective-permute-start | bytes 7077896 | tf_op jit(solution)/shard_map/while/body/eval_jaxpr/ppermute | solution.py:330
  1488.5 34.5 collective-permute-start.1
  1506.4 16.6 collective-permute-start
  1531.1 140.9 %collective-permute-start.2 = (bf16[768,1536]{1,0:T(8,128)(2,1)}, bf16[768,1536]{1,0:T(8,128)(2,1)}, u32[]{:S(2)}, u32[]{:S(2)}) collective-permute-start(bf16[768,1536]{1,0:T(8,128)(2,1)} %get-tuple-element.1636), channel_id=1, source_target_pairs={{0,4},{3,7},{4,0},{7,3}} | collective-permute-start | bytes 7077896 | tf_op jit(solution)/shard_map/while/body/eval_jaxpr/ppermute | solution.py:330
  1640.6 34.6 collective-permute-start.1
  1658.6 16.6 collective-permute-start
  1683.3 140.8 %collective-permute-start.2 = (bf16[768,1536]{1,0:T(8,128)(2,1)}, bf16[768,1536]{1,0:T(8,128)(2,1)}, u32[]{:S(2)}, u32[]{:S(2)}) collective-permute-start(bf16[768,1536]{1,0:T(8,128)(2,1)} %get-tuple-element.1636), channel_id=1, source_target_pairs={{0,4},{3,7},{4,0},{7,3}} | collective-permute-start | bytes 7077896 | tf_op jit(solution)/shard_map/while/body/eval_jaxpr/ppermute | solution.py:330
  1792.7 34.6 collective-permute-start.1
  1810.7 16.6 collective-permute-start
  1845.1 147.6 %collective-permute-start.3 = (bf16[768,1536]{1,0:T(8,128)(2,1)}, bf16[768,1536]{1,0:T(8,128)(2,1)}, u32[]{:S(2)}, u32[]{:S(2)}) collective-permute-start(bf16[768,1536]{1,0:T(8,128)(2,1)} %broadcast_select_fusion.14), channel_id=1, source_target_pairs={{0,1},{1,2},{2,3},{4,5},{5,6},{6,7}} | collective-permute-start | bytes 7077896 | tf_op jit(solution)/shard_map/while/body/eval_jaxpr/ppermute | solution.py:365
  1863.1 136.1 %collective-permute-start.5 = (bf16[768,1536]{1,0:T(8,128)(2,1)}, bf16[768,1536]{1,0:T(8,128)(2,1)}, u32[]{:S(2)}, u32[]{:S(2)}) collective-permute-start(bf16[768,1536]{1,0:T(8,128)(2,1)} %broadcast_select_fusion.15), channel_id=1, source_target_pairs={{2,1},{6,5}} | collective-permute-start | bytes 7077896 | tf_op jit(solution)/shard_map/while/body/eval_jaxpr/ppermute | solution.py:366
  2012.1 136.9 %collective-permute-start.3 = (bf16[768,1536]{1,0:T(8,128)(2,1)}, bf16[768,1536]{1,0:T(8,128)(2,1)}, u32[]{:S(2)}, u32[]{:S(2)}) collective-permute-start(bf16[768,1536]{1,0:T(8,128)(2,1)} %broadcast_select_fusion.14), channel_id=1, source_target_pairs={{0,1},{1,2},{2,3},{4,5},{5,6},{6,7}} | collective-permute-start | bytes 7077896 | tf_op jit(solution)/shard_map/while/body/eval_jaxpr/ppermute | solution.py:365
  2018.7 136.8 %collective-permute-start.5 = (bf16[768,1536]{1,0:T(8,128)(2,1)}, bf16[768,1536]{1,0:T(8,128)(2,1)}, u32[]{:S(2)}, u32[]{:S(2)}) collective-permute-start(bf16[768,1536]{1,0:T(8,128)(2,1)} %broadcast_select_fusion.15), channel_id=1, source_target_pairs={{2,1},{6,5}} | collective-permute-start | bytes 7077896 | tf_op jit(solution)/shard_map/while/body/eval_jaxpr/ppermute | solution.py:366
  2169.8 136.9 %collective-permute-start.3 = (bf16[768,1536]{1,0:T(8,128)(2,1)}, bf16[768,1536]{1,0:T(8,128)(2,1)}, u32[]{:S(2)}, u32[]{:S(2)}) collective-permute-start(bf16[768,1536]{1,0:T(8,128)(2,1)} %broadcast_select_fusion.14), channel_id=1, source_target_pairs={{0,1},{1,2},{2,3},{4,5},{5,6},{6,7}} | collective-permute-start | bytes 7077896 | tf_op jit(solution)/shard_map/while/body/eval_jaxpr/ppermute | solution.py:365
  2176.5 136.8 %collective-permute-start.5 = (bf16[768,1536]{1,0:T(8,128)(2,1)}, bf16[768,1536]{1,0:T(8,128)(2,1)}, u32[]{:S(2)}, u32[]{:S(2)}) collective-permute-start(bf16[768,1536]{1,0:T(8,128)(2,1)} %broadcast_select_fusion.15), channel_id=1, source_target_pairs={{2,1},{6,5}} | collective-permute-start | bytes 7077896 | tf_op jit(solution)/shard_map/while/body/eval_jaxpr/ppermute | solution.py:366
  2327.9 136.9 %collective-permute-start.3 = (bf16[768,1536]{1,0:T(8,128)(2,1)}, bf16[768,1536]{1,0:T(8,128)(2,1)}, u32[]{:S(2)}, u32[]{:S(2)}) collective-permute-start(bf16[768,1536]{1,0:T(8,128)(2,1)} %broadcast_select_fusion.14), channel_id=1, source_target_pairs={{0,1},{1,2},{2,3},{4,5},{5,6},{6,7}} | collective-permute-start | bytes 7077896 | tf_op jit(solution)/shard_map/while/body/eval_jaxpr/ppermute | solution.py:365
  2334.6 136.8 %collective-permute-start.5 = (bf16[768,1536]{1,0:T(8,128)(2,1)}, bf16[768,1536]{1,0:T(8,128)(2,1)}, u32[]{:S(2)}, u32[]{:S(2)}) collective-permute-start(bf16[768,1536]{1,0:T(8,128)(2,1)} %broadcast_select_fusion.15), channel_id=1, source_target_pairs={{2,1},{6,5}} | collective-permute-start | bytes 7077896 | tf_op jit(solution)/shard_map/while/body/eval_jaxpr/ppermute | solution.py:366
  2470.1 8.7 collective-permute-start.4
  2486.2 136.9 %collective-permute-start.3 = (bf16[768,1536]{1,0:T(8,128)(2,1)}, bf16[768,1536]{1,0:T(8,128)(2,1)}, u32[]{:S(2)}, u32[]{:S(2)}) collective-permute-start(bf16[768,1536]{1,0:T(8,128)(2,1)} %broadcast_select_fusion.14), channel_id=1, source_target_pairs={{0,1},{1,2},{2,3},{4,5},{5,6},{6,7}} | collective-permute-start | bytes 7077896 | tf_op jit(solution)/shard_map/while/body/eval_jaxpr/ppermute | solution.py:365
  2492.9 136.8 %collective-permute-start.5 = (bf16[768,1536]{1,0:T(8,128)(2,1)}, bf16[768,1536]{1,0:T(8,128)(2,1)}, u32[]{:S(2)}, u32[]{:S(2)}) collective-permute-start(bf16[768,1536]{1,0:T(8,128)(2,1)} %broadcast_select_fusion.15), channel_id=1, source_target_pairs={{2,1},{6,5}} | collective-permute-start | bytes 7077896 | tf_op jit(solution)/shard_map/while/body/eval_jaxpr/ppermute | solution.py:366
  2628.4 8.8 collective-permute-start.4
  2644.6 137.0 %collective-permute-start.3 = (bf16[768,1536]{1,0:T(8,128)(2,1)}, bf16[768,1536]{1,0:T(8,128)(2,1)}, u32[]{:S(2)}, u32[]{:S(2)}) collective-permute-start(bf16[768,1536]{1,0:T(8,128)(2,1)} %broadcast_select_fusion.14), channel_id=1, source_target_pairs={{0,1},{1,2},{2,3},{4,5},{5,6},{6,7}} | collective-permute-start | bytes 7077896 | tf_op jit(solution)/shard_map/while/body/eval_jaxpr/ppermute | solution.py:365
  2651.3 136.9 %collective-permute-start.5 = (bf16[768,1536]{1,0:T(8,128)(2,1)}, bf16[768,1536]{1,0:T(8,128)(2,1)}, u32[]{:S(2)}, u32[]{:S(2)}) collective-permute-start(bf16[768,1536]{1,0:T(8,128)(2,1)} %broadcast_select_fusion.15), channel_id=1, source_target_pairs={{2,1},{6,5}} | collective-permute-start | bytes 7077896 | tf_op jit(solution)/shard_map/while/body/eval_jaxpr/ppermute | solution.py:366
  2802.8 137.0 %collective-permute-start.3 = (bf16[768,1536]{1,0:T(8,128)(2,1)}, bf16[768,1536]{1,0:T(8,128)(2,1)}, u32[]{:S(2)}, u32[]{:S(2)}) collective-permute-start(bf16[768,1536]{1,0:T(8,128)(2,1)} %broadcast_select_fusion.14), channel_id=1, source_target_pairs={{0,1},{1,2},{2,3},{4,5},{5,6},{6,7}} | collective-permute-start | bytes 7077896 | tf_op jit(solution)/shard_map/while/body/eval_jaxpr/ppermute | solution.py:365
  2809.5 136.9 %collective-permute-start.5 = (bf16[768,1536]{1,0:T(8,128)(2,1)}, bf16[768,1536]{1,0:T(8,128)(2,1)}, u32[]{:S(2)}, u32[]{:S(2)}) collective-permute-start(bf16[768,1536]{1,0:T(8,128)(2,1)} %broadcast_select_fusion.15), channel_id=1, source_target_pairs={{2,1},{6,5}} | collective-permute-start | bytes 7077896 | tf_op jit(solution)/shard_map/while/body/eval_jaxpr/ppermute | solution.py:366
  2961.0 136.9 %collective-permute-start.3 = (bf16[768,1536]{1,0:T(8,128)(2,1)}, bf16[768,1536]{1,0:T(8,128)(2,1)}, u32[]{:S(2)}, u32[]{:S(2)}) collective-permute-start(bf16[768,1536]{1,0:T(8,128)(2,1)} %broadcast_select_fusion.14), channel_id=1, source_target_pairs={{0,1},{1,2},{2,3},{4,5},{5,6},{6,7}} | collective-permute-start | bytes 7077896 | tf_op jit(solution)/shard_map/while/body/eval_jaxpr/ppermute | solution.py:365
  2967.6 136.8 %collective-permute-start.5 = (bf16[768,1536]{1,0:T(8,128)(2,1)}, bf16[768,1536]{1,0:T(8,128)(2,1)}, u32[]{:S(2)}, u32[]{:S(2)}) collective-permute-start(bf16[768,1536]{1,0:T(8,128)(2,1)} %broadcast_select_fusion.15), channel_id=1, source_target_pairs={{2,1},{6,5}} | collective-permute-start | bytes 7077896 | tf_op jit(solution)/shard_map/while/body/eval_jaxpr/ppermute | solution.py:366
  3103.1 8.8 collective-permute-start.4
  3119.3 137.1 %collective-permute-start.3 = (bf16[768,1536]{1,0:T(8,128)(2,1)}, bf16[768,1536]{1,0:T(8,128)(2,1)}, u32[]{:S(2)}, u32[]{:S(2)}) collective-permute-start(bf16[768,1536]{1,0:T(8,128)(2,1)} %broadcast_select_fusion.14), channel_id=1, source_target_pairs={{0,1},{1,2},{2,3},{4,5},{5,6},{6,7}} | collective-permute-start | bytes 7077896 | tf_op jit(solution)/shard_map/while/body/eval_jaxpr/ppermute | solution.py:365
  3126.0 137.0 %collective-permute-start.5 = (bf16[768,1536]{1,0:T(8,128)(2,1)}, bf16[768,1536]{1,0:T(8,128)(2,1)}, u32[]{:S(2)}, u32[]{:S(2)}) collective-permute-start(bf16[768,1536]{1,0:T(8,128)(2,1)} %broadcast_select_fusion.15), channel_id=1, source_target_pairs={{2,1},{6,5}} | collective-permute-start | bytes 7077896 | tf_op jit(solution)/shard_map/while/body/eval_jaxpr/ppermute | solution.py:366
  3277.2 136.9 %collective-permute-start.3 = (bf16[768,1536]{1,0:T(8,128)(2,1)}, bf16[768,1536]{1,0:T(8,128)(2,1)}, u32[]{:S(2)}, u32[]{:S(2)}) collective-permute-start(bf16[768,1536]{1,0:T(8,128)(2,1)} %broadcast_select_fusion.14), channel_id=1, source_target_pairs={{0,1},{1,2},{2,3},{4,5},{5,6},{6,7}} | collective-permute-start | bytes 7077896 | tf_op jit(solution)/shard_map/while/body/eval_jaxpr/ppermute | solution.py:365
  3283.9 136.8 %collective-permute-start.5 = (bf16[768,1536]{1,0:T(8,128)(2,1)}, bf16[768,1536]{1,0:T(8,128)(2,1)}, u32[]{:S(2)}, u32[]{:S(2)}) collective-permute-start(bf16[768,1536]{1,0:T(8,128)(2,1)} %broadcast_select_fusion.15), channel_id=1, source_target_pairs={{2,1},{6,5}} | collective-permute-start | bytes 7077896 | tf_op jit(solution)/shard_map/while/body/eval_jaxpr/ppermute | solution.py:366
  3419.4 8.8 collective-permute-start.4
  3435.6 137.0 %collective-permute-start.3 = (bf16[768,1536]{1,0:T(8,128)(2,1)}, bf16[768,1536]{1,0:T(8,128)(2,1)}, u32[]{:S(2)}, u32[]{:S(2)}) collective-permute-start(bf16[768,1536]{1,0:T(8,128)(2,1)} %broadcast_select_fusion.14), channel_id=1, source_target_pairs={{0,1},{1,2},{2,3},{4,5},{5,6},{6,7}} | collective-permute-start | bytes 7077896 | tf_op jit(solution)/shard_map/while/body/eval_jaxpr/ppermute | solution.py:365
  3442.2 136.8 %collective-permute-start.5 = (bf16[768,1536]{1,0:T(8,128)(2,1)}, bf16[768,1536]{1,0:T(8,128)(2,1)}, u32[]{:S(2)}, u32[]{:S(2)}) collective-permute-start(bf16[768,1536]{1,0:T(8,128)(2,1)} %broadcast_select_fusion.15), channel_id=1, source_target_pairs={{2,1},{6,5}} | collective-permute-start | bytes 7077896 | tf_op jit(solution)/shard_map/while/body/eval_jaxpr/ppermute | solution.py:366
  3593.9 137.0 %collective-permute-start.3 = (bf16[768,1536]{1,0:T(8,128)(2,1)}, bf16[768,1536]{1,0:T(8,128)(2,1)}, u32[]{:S(2)}, u32[]{:S(2)}) collective-permute-start(bf16[768,1536]{1,0:T(8,128)(2,1)} %broadcast_select_fusion.14), channel_id=1, source_target_pairs={{0,1},{1,2},{2,3},{4,5},{5,6},{6,7}} | collective-permute-start | bytes 7077896 | tf_op jit(solution)/shard_map/while/body/eval_jaxpr/ppermute | solution.py:365
  3600.6 136.9 %collective-permute-start.5 = (bf16[768,1536]{1,0:T(8,128)(2,1)}, bf16[768,1536]{1,0:T(8,128)(2,1)}, u32[]{:S(2)}, u32[]{:S(2)}) collective-permute-start(bf16[768,1536]{1,0:T(8,128)(2,1)} %broadcast_select_fusion.15), channel_id=1, source_target_pairs={{2,1},{6,5}} | collective-permute-start | bytes 7077896 | tf_op jit(solution)/shard_map/while/body/eval_jaxpr/ppermute | solution.py:366
  (201 other events, 3370.8 us)
